TPU v7x, 256 devices: a whole 4x4x8 slice. The times are simulated.
256 devices in a mesh: dp: 4 (over y_hi, core), expert: 64 (over z, y_lo, x).
Axes of the slice: x: 4, y: 4 (y_hi: 2, y_lo: 2; y = y_hi * 2 + y_lo), z: 8, core: 2. Of those that a mesh axis runs over, the one named last changes fastest.
Arguments:
- student_latent: bfloat16 [32768, 1024], P(('dp', 'expert')), may hold values from -6 to 6
- target_latent: bfloat16 [32768, 1024], P(('dp', 'expert')), may hold values from -6 to 6
- student_gate: bfloat16 [64, 1024, 2048], P('expert', None, 'dp'), may hold values from -0.1875 to 0.1875
- student_up: bfloat16 [64, 1024, 2048], P('expert', None, 'dp'), may hold values from -0.1875 to 0.1875
- student_down: bfloat16 [64, 2048, 1024], P('expert', 'dp'), may hold values from -0.125 to 0.125
- target_gate: bfloat16 [64, 1024, 2048], P('expert', None, 'dp'), may hold values from -0.1875 to 0.1875
- target_up: bfloat16 [64, 1024, 2048], P('expert', None, 'dp'), may hold values from -0.1875 to 0.1875
- target_down: bfloat16 [64, 2048, 1024], P('expert', 'dp'), may hold values from -0.125 to 0.125
- student_routes: int32 [32768, 2], P(('dp', 'expert')), may hold values from 0 to 63, all different within a row; in each aligned block of 128 rows (0 to 127, 128 to 255, ...) at most 5 rows name the same one
- target_routes: int32 [32768, 2], P(('dp', 'expert')), may hold values from 0 to 63, all different within a row; in each aligned block of 128 rows (0 to 127, 128 to 255, ...) at most 5 rows name the same one
- student_mixing: float32 [32768, 2], P(('dp', 'expert')), may hold values from 0.1 to 1
- target_mixing: float32 [32768, 2], P(('dp', 'expert')), may hold values from 0.1 to 1
Outputs:
- gate_gradient: bfloat16 [64, 1024, 2048], P('expert', None, 'dp')
- up_gradient: bfloat16 [64, 1024, 2048], P('expert', None, 'dp')
- down_gradient: bfloat16 [64, 2048, 1024], P('expert', 'dp')
Inputs may be any that keep to these rules, and one draw needn't show every extreme that they name: `student_routes`: each row names 2 different experts; within the 128 rows of one device (aligned blocks) no expert is named more than 5 times, a bound that some block reaches. `target_routes`: each row names 2 different experts; within the 128 rows of one device (aligned blocks) no expert is named more than 5 times, a bound that some block reaches.
All inputs are finite; a program needn't handle non-finite values.
Results may differ from a plain program's by a relative error of at most 0.012.
Values may be sent and summed in bfloat16 or wider, within the bound.
No kernel may reach another device: no remote copies, remote signals or barrier semaphores. Data moves between devices by JAX's collectives and lax.ppermute only.
A program may use at most 128 MiB of HBM per device.

v0:
```python
import jax
import jax.numpy as jnp
from jax import lax
from jax.sharding import PartitionSpec as P


def sent_together(arrays, axis, dim, along):
    ends, at = ([], 0)
    for a in arrays[:-1]:
        at += a.shape[along]
        ends.append(at)
    both = jnp.concatenate(arrays, axis=along)
    return tuple(jnp.split(lax.all_gather(both, axis, axis=dim, tiled=True), ends, axis=along))


def rms_rows(latent):
    widened = latent.astype(jnp.float32)
    factor = lax.rsqrt(jnp.mean(widened * widened, axis=1, keepdims=True) + 1e-06)
    return (widened * factor).astype(jnp.bfloat16)


def slot_tables(routes, experts, capacity):
    labels = routes.reshape(-1)
    total_rows = labels.shape[0]
    experts_list = jnp.arange(experts, dtype=jnp.int32)
    onehot = (labels[:, None] == experts_list[None, :]).astype(jnp.int32)
    before = jnp.cumsum(onehot, axis=0) - onehot
    position = jnp.sum(before * onehot, axis=1)
    placed = labels * capacity + position
    source = jnp.full((experts * capacity,), total_rows, jnp.int32)
    source = source.at[placed].set(jnp.arange(total_rows, dtype=jnp.int32))
    return (placed, source)


def pack_rows(values, source):
    padded = jnp.concatenate([values, jnp.zeros((1, values.shape[1]), values.dtype)], axis=0)
    return jnp.take(padded, source, axis=0)


def expert_forward(arrived, weight_gate, weight_up, weight_down):
    pre_gate = jnp.dot(arrived, weight_gate, preferred_element_type=jnp.float32)
    pre_up = jnp.dot(arrived, weight_up, preferred_element_type=jnp.float32)
    hidden = (jax.nn.silu(pre_gate) * pre_up).astype(jnp.bfloat16)
    partial_sum = jnp.dot(hidden, weight_down, preferred_element_type=jnp.float32)
    return (pre_gate, pre_up, hidden, partial_sum)


def send_pair(student_rows, target_rows):
    received = (
        lax.all_to_all(student_rows, "expert", split_axis=0, concat_axis=0, tiled=True),
        lax.all_to_all(target_rows, "expert", split_axis=0, concat_axis=0, tiled=True),
    )
    return sent_together((received[0], received[1]), "dp", 0, 1)


def return_pair(student_sum, target_sum):
    summed = (
        lax.psum_scatter(
            student_sum.astype(jnp.bfloat16), "dp", scatter_dimension=0, tiled=True
        ).astype(jnp.float32),
        lax.psum_scatter(
            target_sum.astype(jnp.bfloat16), "dp", scatter_dimension=0, tiled=True
        ).astype(jnp.float32),
    )
    rounded_student = summed[0].astype(jnp.bfloat16)
    rounded_target = summed[1].astype(jnp.bfloat16)
    return (
        lax.all_to_all(rounded_student, "expert", split_axis=0, concat_axis=0, tiled=True),
        lax.all_to_all(rounded_target, "expert", split_axis=0, concat_axis=0, tiled=True),
    )


def combine_rows(latent, mixing, placed, outputs):
    picked = jnp.take(outputs, placed, axis=0).reshape(
        latent.shape[0], mixing.shape[1], latent.shape[1]
    )
    return latent.astype(jnp.float32) + jnp.sum(
        mixing[:, :, None] * picked.astype(jnp.float32), axis=1
    )


def shards(
    student_latent,
    target_latent,
    student_gate,
    student_up,
    student_down,
    target_gate,
    target_up,
    target_down,
    student_routes,
    target_routes,
    student_mixing,
    target_mixing,
):
    groups = lax.axis_size("dp")
    experts = lax.axis_size("expert")
    tokens_here = student_latent.shape[0]
    top_count = student_routes.shape[1]
    feature_width = student_latent.shape[1]
    capacity = tokens_here * top_count * 5 // (4 * experts)
    normed_student = rms_rows(student_latent)
    normed_target = rms_rows(target_latent)
    placed_student, source_student = slot_tables(student_routes, experts, capacity)
    placed_target, source_target = slot_tables(target_routes, experts, capacity)
    outgoing_student = pack_rows(normed_student, source_student // top_count)
    outgoing_target = pack_rows(normed_target, source_target // top_count)
    arrived = send_pair(outgoing_student, outgoing_target)
    pre_gate, pre_up, hidden, student_sum = expert_forward(
        arrived[0], student_gate[0], student_up[0], student_down[0]
    )
    target_sum = expert_forward(arrived[1], target_gate[0], target_up[0], target_down[0])[3]
    results = return_pair(student_sum, target_sum)
    student_out = combine_rows(student_latent, student_mixing, placed_student, results[0])
    target_out = combine_rows(target_latent, target_mixing, placed_target, results[1])
    factor = (experts / (top_count * tokens_here * groups * experts)) ** 0.5
    cotangent = factor * (student_out - target_out)
    slot_values = (
        (student_mixing[:, :, None] * cotangent[:, None, :])
        .astype(jnp.bfloat16)
        .reshape(-1, feature_width)
    )
    outgoing_slots = pack_rows(slot_values, source_student)
    received_slots = lax.all_to_all(
        outgoing_slots, "expert", split_axis=0, concat_axis=0, tiled=True
    )
    slot_cotangent = lax.all_gather(received_slots, "dp", axis=0, tiled=True)
    down_part = lax.dot_general(
        hidden, slot_cotangent, (((0,), (0,)), ((), ())), preferred_element_type=jnp.float32
    )
    grad_hidden = lax.dot_general(
        slot_cotangent,
        student_down[0],
        (((1,), (1,)), ((), ())),
        preferred_element_type=jnp.float32,
    )
    sigmoid_gate = jax.nn.sigmoid(pre_gate)
    grad_pre_gate = (
        grad_hidden * pre_up * sigmoid_gate * (1.0 + pre_gate * (1.0 - sigmoid_gate))
    ).astype(jnp.bfloat16)
    grad_pre_up = (grad_hidden * pre_gate * sigmoid_gate).astype(jnp.bfloat16)
    gate_part = lax.dot_general(
        arrived[0], grad_pre_gate, (((0,), (0,)), ((), ())), preferred_element_type=jnp.float32
    )
    up_part = lax.dot_general(
        arrived[0], grad_pre_up, (((0,), (0,)), ((), ())), preferred_element_type=jnp.float32
    )
    return (
        gate_part.astype(jnp.bfloat16)[None],
        up_part.astype(jnp.bfloat16)[None],
        down_part.astype(jnp.bfloat16)[None],
    )


def solution(mesh):
    in_specs = (
        P(("dp", "expert"), None),
        P(("dp", "expert"), None),
        P("expert", None, "dp"),
        P("expert", None, "dp"),
        P("expert", "dp", None),
        P("expert", None, "dp"),
        P("expert", None, "dp"),
        P("expert", "dp", None),
        P(("dp", "expert"), None),
        P(("dp", "expert"), None),
        P(("dp", "expert"), None),
        P(("dp", "expert"), None),
    )
    out_specs = (P("expert", None, "dp"), P("expert", None, "dp"), P("expert", "dp", None))
    return jax.shard_map(shards, mesh=mesh, in_specs=in_specs, out_specs=out_specs, check_vma=False)
```

profile of v0, /device:TPU:1, one launch (start us, length us, event | category | flops | bytes accessed | tf_op | source)
XLA Modules:
  0.0 385.4 jit_solution(6882959379181185574)
XLA Ops:
  11.4 1.4 scatter_custom_fusion.1
  13.9 2.1 gather_fusion.2
  17.4 13.5 %all-to-all-start.1 = ((bf16[64,5,1024]{2,1,0:T(8,128)(2,1)}), bf16[64,5,1024]{2,1,0:T(8,128)(2,1)S(1)}, u32[]{:S(2)}, u32[]{:S(2)}) async-start(bf16[64,5,1024]{2,1,0:T(8,128)(2,1)} %all_to_all.41), calls=%async_computation.1 | async-start | bytes 2097152 | tf_op jit(solution)/shard_map/all_to_all | solution.py:51
  32.9 1.4 scatter_custom_fusion
  34.3 2.1 gather_fusion.1
  37.8 19.2 %all-to-all-done.1 = bf16[64,5,1024]{2,1,0:T(8,128)(2,1)S(1)} async-done(((bf16[64,5,1024]{2,1,0:T(8,128)(2,1)}), bf16[64,5,1024]{2,1,0:T(8,128)(2,1)S(1)}, u32[]{:S(2)}, u32[]{:S(2)}) %all-to-all-start.1) | async-done | bytes 655392 | tf_op jit(solution)/shard_map/all_to_all | solution.py:51
  57.0 7.7 %all-to-all-start = ((bf16[64,5,1024]{2,1,0:T(8,128)(2,1)}), bf16[64,5,1024]{2,1,0:T(8,128)(2,1)S(1)}, u32[]{:S(2)}, u32[]{:S(2)}) async-start(bf16[64,5,1024]{2,1,0:T(8,128)(2,1)} %all_to_all.38), calls=%async_computation | async-start | bytes 2097152 | tf_op jit(solution)/shard_map/all_to_all | solution.py:50
  65.9 23.8 %all-to-all-done = bf16[64,5,1024]{2,1,0:T(8,128)(2,1)S(1)} async-done(((bf16[64,5,1024]{2,1,0:T(8,128)(2,1)}), bf16[64,5,1024]{2,1,0:T(8,128)(2,1)S(1)}, u32[]{:S(2)}, u32[]{:S(2)}) %all-to-all-start) | async-done | bytes 655392 | tf_op jit(solution)/shard_map/all_to_all | solution.py:50
  90.0 2.4 pad_maximum_fusion
  92.7 48.2 %all-gather.3.cloned.1.call-done = bf16[1280,2048]{1,0:T(8,128)(2,1)} async-done(((bf16[320,2048]{1,0:T(8,128)(2,1)}), bf16[1280,2048]{1,0:T(8,128)(2,1)}) %all-gather.3.cloned.1.call-update) | async-done | bytes 5242896 | tf_op jit(solution)/shard_map/all_gather | solution.py:13
  140.8 4.7 %fusion.2 = f32[1280,512]{1,0:T(8,128)} fusion(bf16[1280,2048]{1,0:T(8,128)(2,1)} %all-gather.3.cloned.1.call-done, bf16[1,1024,512]{2,1,0:T(8,128)(2,1)S(1)} %copy-done.17), kind=kOutput, calls=%fused_computation.16 | convolution fusion | flops 1342177280 | bytes 6291456 | tf_op jit(solution)/shard_map/dot_general | solution.py:41
  145.6 7.7 %convolution_convert_fusion = bf16[1280,1024]{1,0:T(8,128)(2,1)} fusion(f32[1280,512]{1,0:T(8,128)} %fusion.2, bf16[1280,2048]{1,0:T(8,128)(2,1)} %all-gather.3.cloned.1.call-done, bf16[1,512,1024]{2,1,0:T(8,128)(2,1)} %param.23, bf16[1,1024,512]{2,1,0:T(8,128)(2,1)} %param.22), kind=kOutput, calls=%fused_computation.7 | convolution fusion | flops 2689597440 | bytes 9961472 | tf_op jit(solution)/shard_map/dot_general | solution.py:44
  154.5 3.3 fusion.10
  157.8 6.1 %multiply_convert_fusion.2 = (bf16[1280,512]{1,0:T(8,128)(2,1)S(1)}, f32[1280,512]{1,0:T(8,128)}) fusion(f32[1280,512]{1,0:T(8,128)S(1)} %fusion.10, bf16[1,1024,512]{2,1,0:T(8,128)(2,1)S(1)} %copy-done.19, bf16[1280,2048]{1,0:T(8,128)(2,1)} %all-gather.3.cloned.1.call-done), kind=kOutput, calls=%fused_computation.13 | convolution fusion | flops 1346109440 | bytes 10223616 | tf_op jit(solution)/shard_map/dot_general | solution.py:42
  165.0 3.0 convolution_convert_fusion.1
  168.0 30.9 %reduce-scatter.5.cloned.1.call-done = bf16[320,1024]{1,0:T(8,128)(2,1)} async-done(((bf16[1280,1024]{1,0:T(8,128)(2,1)}), bf16[320,1024]{1,0:T(8,128)(2,1)}) %reduce-scatter.5.cloned.1.call-update) | async-done | bytes 655376 | tf_op jit(solution)/shard_map/reduce_scatter | solution.py:61
  198.9 2.1 all_to_all.47
  201.0 10.3 %all-to-all-start.3 = ((bf16[64,5,1024]{2,1,0:T(8,128)(2,1)}), bf16[64,5,1024]{2,1,0:T(8,128)(2,1)S(1)}, u32[]{:S(2)}, u32[]{:S(2)}) async-start(bf16[64,5,1024]{2,1,0:T(8,128)(2,1)} %all_to_all.47), calls=%async_computation.5 | async-start | bytes 2097152 | tf_op jit(solution)/shard_map/all_to_all | solution.py:69
  211.3 39.1 %reduce-scatter.3.cloned.1.call-done = bf16[320,1024]{1,0:T(8,128)(2,1)} async-done(((bf16[1280,1024]{1,0:T(8,128)(2,1)}), bf16[320,1024]{1,0:T(8,128)(2,1)}) %reduce-scatter.3.cloned.1.call-update) | async-done | bytes 655376 | tf_op jit(solution)/shard_map/reduce_scatter | solution.py:58
  250.5 2.1 all_to_all.44
  252.6 9.4 %all-to-all-start.2 = ((bf16[64,5,1024]{2,1,0:T(8,128)(2,1)}), bf16[64,5,1024]{2,1,0:T(8,128)(2,1)}, u32[]{:S(2)}, u32[]{:S(2)}) async-start(bf16[64,5,1024]{2,1,0:T(8,128)(2,1)} %all_to_all.44), calls=%async_computation.3 | async-start | bytes 2097152 | tf_op jit(solution)/shard_map/all_to_all | solution.py:68
  265.8 22.3 %all-to-all-done.2 = bf16[64,5,1024]{2,1,0:T(8,128)(2,1)} async-done(((bf16[64,5,1024]{2,1,0:T(8,128)(2,1)}), bf16[64,5,1024]{2,1,0:T(8,128)(2,1)}, u32[]{:S(2)}, u32[]{:S(2)}) %all-to-all-start.2) | async-done | bytes 655392 | tf_op jit(solution)/shard_map/all_to_all | solution.py:68
  288.0 1.4 all_to_all.46
  291.8 1.9 reshape.160
  293.7 2.7 multiply_reduce_fusion
  297.8 2.1 gather_fusion
  300.3 32.6 %all_to_all.57 = bf16[64,5,1024]{2,1,0:T(8,128)(2,1)S(1)} all-to-all(bf16[64,5,1024]{2,1,0:T(8,128)(2,1)S(1)} %broadcast_select_fusion), channel_id=1, replica_groups=mesh['dp'=4,'expert'=64] {'expert'}, dimensions={0} | all-to-all | bytes 1310720 | tf_op jit(solution)/shard_map/all_to_all | solution.py:124
  334.1 32.9 %all-gather.5.cloned.1.call-done = bf16[1280,1024]{1,0:T(8,128)(2,1)} async-done(((bf16[320,1024]{1,0:T(8,128)(2,1)}), bf16[1280,1024]{1,0:T(8,128)(2,1)}) %all-gather.5.cloned.1.call-update) | async-done | bytes 2621456 | tf_op jit(solution)/shard_map/all_gather | solution.py:127
  367.1 4.4 %fusion.18 = bf16[1,512,1024]{2,1,0:T(8,128)(2,1)} fusion(bf16[1280,512]{1,0:T(8,128)(2,1)S(1)} %copy-done.6, bf16[1280,1024]{1,0:T(8,128)(2,1)} %all-gather.5.cloned.1.call-done), kind=kOutput, calls=%fused_computation.29 | convolution fusion | flops 1342701568 | bytes 4980736 | tf_op jit(solution)/shard_map/dot_general | solution.py:128
  371.5 1.6 fusion.31
  373.5 2.6 fusion.19
  376.1 2.7 fusion.22
  (130 shorter events, 23.2 us)
Async XLA Ops:
  7.2 157.8 %copy-start = (bf16[1,512,1024]{2,1,0:T(8,128)(2,1)S(1)}, bf16[1,512,1024]{2,1,0:T(8,128)(2,1)}, u32[]{:S(2)}) copy-start(bf16[1,512,1024]{2,1,0:T(8,128)(2,1)} %param.20) | copy-start | bytes 3145732
  11.3 1.5 copy-start.9
  16.0 14.9 %copy-start.13 = (s32[128,2]{0,1:T(2,128)S(1)}, s32[128,2]{0,1:T(2,128)}, u32[]{:S(2)}) copy-start(s32[128,2]{0,1:T(2,128)} %param.24) | copy-start | bytes 3076
  16.0 15.3 %copy-start.3 = (bf16[128,1024]{1,0:T(8,128)(2,1)S(1)}, bf16[128,1024]{1,0:T(8,128)(2,1)}, u32[]{:S(2)}) copy-start(bf16[128,1024]{1,0:T(8,128)(2,1)} %param.16) | copy-start | bytes 786436
  17.4 39.6 %all-to-all-start.1 = ((bf16[64,5,1024]{2,1,0:T(8,128)(2,1)}), bf16[64,5,1024]{2,1,0:T(8,128)(2,1)S(1)}, u32[]{:S(2)}, u32[]{:S(2)}) async-start(bf16[64,5,1024]{2,1,0:T(8,128)(2,1)} %all_to_all.41), calls=%async_computation.1 | async-start | bytes 2097152 | tf_op jit(solution)/shard_map/all_to_all | solution.py:51
  31.2 5.2 %copy-start.7 = (s32[256]{0:T(256)}, s32[256]{0:T(256)S(1)}, u32[]{:S(2)}) copy-start(s32[256]{0:T(256)S(1)} %eq.50) | copy-start | bytes 3076
  32.8 3.6 copy-start.11
  57.0 32.7 %all-to-all-start = ((bf16[64,5,1024]{2,1,0:T(8,128)(2,1)}), bf16[64,5,1024]{2,1,0:T(8,128)(2,1)S(1)}, u32[]{:S(2)}, u32[]{:S(2)}) async-start(bf16[64,5,1024]{2,1,0:T(8,128)(2,1)} %all_to_all.38), calls=%async_computation | async-start | bytes 2097152 | tf_op jit(solution)/shard_map/all_to_all | solution.py:50
  64.7 76.1 %all-gather.3.cloned.1.call-start = ((), (), s32[]{:S(2)}) async-start(), calls=%async_computation.7 | async-start | bytes 6553600 | tf_op jit(solution)/shard_map/all_gather | solution.py:13
  90.0 50.8 %copy-start.17 = (bf16[1,1024,512]{2,1,0:T(8,128)(2,1)S(1)}, bf16[1,1024,512]{2,1,0:T(8,128)(2,1)}, u32[]{:S(2)}) copy-start(bf16[1,1024,512]{2,1,0:T(8,128)(2,1)} %param.21) | copy-start | bytes 3145732
  92.5 106.4 %reduce-scatter.5.cloned.1.call-start = ((), (), s32[]{:S(2)}) async-start(), calls=%async_computation.9 | async-start | bytes 3276800 | tf_op jit(solution)/shard_map/reduce_scatter | solution.py:61
  153.3 1.2 copy-start.18
  153.3 4.5 %copy-start.19 = (bf16[1,1024,512]{2,1,0:T(8,128)(2,1)S(1)}, bf16[1,1024,512]{2,1,0:T(8,128)(2,1)}, u32[]{:S(2)}) copy-start(bf16[1,1024,512]{2,1,0:T(8,128)(2,1)} %param.19) | copy-start | bytes 3145732
  153.3 97.2 %reduce-scatter.3.cloned.1.call-start = ((), (), s32[]{:S(2)}) async-start(), calls=%async_computation.8 | async-start | bytes 3276800 | tf_op jit(solution)/shard_map/reduce_scatter | solution.py:58
  157.8 6.1 %copy-start.20 = (f32[1280,512]{1,0:T(8,128)}, f32[1280,512]{1,0:T(8,128)S(1)}, u32[]{:S(2)}) copy-start(f32[1280,512]{1,0:T(8,128)S(1)} %fusion.10) | copy-start | bytes 7864324
  201.0 61.3 %copy-start.15 = (f32[128,2]{0,1:T(2,128)S(1)}, f32[128,2]{0,1:T(2,128)}, u32[]{:S(2)}) copy-start(f32[128,2]{0,1:T(2,128)} %param.26) | copy-start | bytes 3076
  201.0 62.3 %copy-start.16 = (f32[128,2]{0,1:T(2,128)S(1)}, f32[128,2]{0,1:T(2,128)}, u32[]{:S(2)}) copy-start(f32[128,2]{0,1:T(2,128)} %param.27) | copy-start | bytes 3076
  201.0 62.4 %copy-start.8 = (s32[256]{0:T(256)S(1)}, s32[256]{0:T(256)}, u32[]{:S(2)}) copy-start(s32[256]{0:T(256)} %copy-done.7) | copy-start | bytes 3076
  201.0 62.4 %copy-start.12 = (s32[256]{0:T(256)S(1)}, s32[256]{0:T(256)}, u32[]{:S(2)}) copy-start(s32[256]{0:T(256)} %copy-done.11) | copy-start | bytes 3076
  201.0 62.5 %copy-start.10 = (s32[256]{0:T(256)S(1)}, s32[256]{0:T(256)}, u32[]{:S(2)}) copy-start(s32[256]{0:T(256)} %copy-done.9) | copy-start | bytes 3076
  201.0 51.6 %all-to-all-start.3 = ((bf16[64,5,1024]{2,1,0:T(8,128)(2,1)}), bf16[64,5,1024]{2,1,0:T(8,128)(2,1)S(1)}, u32[]{:S(2)}, u32[]{:S(2)}) async-start(bf16[64,5,1024]{2,1,0:T(8,128)(2,1)} %all_to_all.47), calls=%async_computation.5 | async-start | bytes 2097152 | tf_op jit(solution)/shard_map/all_to_all | solution.py:69
  252.6 35.4 %all-to-all-start.2 = ((bf16[64,5,1024]{2,1,0:T(8,128)(2,1)}), bf16[64,5,1024]{2,1,0:T(8,128)(2,1)}, u32[]{:S(2)}, u32[]{:S(2)}) async-start(bf16[64,5,1024]{2,1,0:T(8,128)(2,1)} %all_to_all.44), calls=%async_computation.3 | async-start | bytes 2097152 | tf_op jit(solution)/shard_map/all_to_all | solution.py:68
  262.0 105.0 %all-gather.5.cloned.1.call-start = ((), (), s32[]{:S(2)}) async-start(), calls=%async_computation.10 | async-start | bytes 3276800 | tf_op jit(solution)/shard_map/all_gather | solution.py:127
  291.8 4.6 %copy-start.2 = (bf16[128,1024]{1,0:T(8,128)(2,1)S(1)}, bf16[128,1024]{1,0:T(8,128)(2,1)}, u32[]{:S(2)}) copy-start(bf16[128,1024]{1,0:T(8,128)(2,1)} %param.17) | copy-start | bytes 786436
  293.6 2.7 copy-start.4
  296.3 1.3 copy-start.14
  300.3 66.7 %copy-start.6 = (bf16[1280,512]{1,0:T(8,128)(2,1)S(1)}, bf16[1280,512]{1,0:T(8,128)(2,1)}, u32[]{:S(2)}) copy-start(bf16[1280,512]{1,0:T(8,128)(2,1)} %copy-done.5) | copy-start | bytes 3932164
  367.0 4.4 %copy-start.1 = (bf16[1280,1024]{1,0:T(8,128)(2,1)S(1)}, bf16[1280,1024]{1,0:T(8,128)(2,1)}, u32[]{:S(2)}) copy-start(bf16[1280,1024]{1,0:T(8,128)(2,1)} %all-gather.5.cloned.1.call-done) | copy-start | bytes 7864324
  367.0 6.0 %slice-start = ((s8[5242880]{0:T(1024)(128)(4,1)}), s8[4194304]{0:T(1024)(128)(4,1)S(1)}, s32[]{:S(2)}) async-start(s8[5242880]{0:T(1024)(128)(4,1)} %bitcast.81), calls=%async_computation.11 | async-start | bytes 8388608
  371.5 1.6 slice-start.1
  371.5 2.1 copy-start.21
  373.5 2.6 copy-start.22
  (1 other events, 1.1 us)
Sparse Core Ops, SparseCore 0:
  92.6 48.2 all-gather.2
  153.4 45.4 reduce-scatter.4
  201.7 48.7 reduce-scatter.2
  334.2 32.7 all-gather.4
where the time goes:
time: 386 us; the launch traced here: 385 us
  waiting for transfers between devices  216 us (56%)
  starting transfers between devices  41.5 us (11%)
  matrix products  36.1 us (9%)
  blocking collectives  32.6 us (8%)
  local copies, waits for them, and re-layouts  32.4 us (8%)
  between operations  14.4 us (4%)
  other arithmetic  11.8 us (3%)
    all_gather x1, waiting for transfers between devices, sent_together(): lax.all_gather(both, axis, axis=dim, tiled=True)  48.2 us
    reduce_scatter x1, waiting for transfers between devices, return_pair(): lax.psum_scatter(student_sum.astype(jnp.bfloat16), 'dp', scatter_dimensio...  39.1 us
    all_gather x1, waiting for transfers between devices, shards(): slot_cotangent = lax.all_gather(received_slots, 'dp', axis=0, tiled=True)  32.9 us
    all_to_all x1, blocking collectives, shards(): lax.all_to_all(outgoing_slots, 'expert', split_axis=0, concat_axis=0, til...  32.6 us
    reduce_scatter x1, waiting for transfers between devices, return_pair(): lax.psum_scatter(target_sum.astype(jnp.bfloat16), 'dp', scatter_dimension...  30.9 us
    all_to_all x1, waiting for transfers between devices, send_pair(): lax.all_to_all(student_rows, 'expert', split_axis=0, concat_axis=0, tiled...  23.8 us
    all_to_all x1, waiting for transfers between devices, return_pair(): lax.all_to_all(rounded_student, 'expert', split_axis=0, concat_axis=0, ti...  22.3 us
    all_to_all x1, waiting for transfers between devices, send_pair(): lax.all_to_all(target_rows, 'expert', split_axis=0, concat_axis=0, tiled=...  19.2 us
  transfers between devices with their start and end apart: 8, of which 7 were waited for; matrix products, arithmetic and copies ran while one was open for 5% of the time, Pallas kernels for 0%

commit v1 on v0

v1 whole, which is shorter than its diff:
```python
import functools
import jax
import jax.numpy as jnp
from jax import lax
from jax.experimental import pallas as pl
from jax.experimental.pallas import tpu as pltpu
from jax.sharding import PartitionSpec as P


F32 = jnp.float32
BF16 = jnp.bfloat16
LANES = 128


def params(mib):
    return pltpu.CompilerParams(vmem_limit_bytes=mib * 1024 * 1024)


def call(body, outs, scratch=(), mib=32, cost=None, **more):
    return pl.pallas_call(
        body,
        out_shape=outs,
        scratch_shapes=list(scratch),
        compiler_params=params(mib),
        cost_estimate=pl.CostEstimate(flops=cost or 1, bytes_accessed=1 << 20, transcendentals=0),
        **more,
    )


def store_flat(value, scratch):
    rows, width = value.shape
    pieces = width // LANES
    for c in range(pieces):
        scratch[pl.ds(c, rows, stride=pieces), :] = value[:, c * LANES : (c + 1) * LANES]


def load_flat(scratch, pieces, c):
    return scratch[pl.ds(c, scratch.shape[0] // pieces, stride=pieces), :]


def column(rows, k):
    n = rows.shape[1]
    return jnp.broadcast_to(rows[k : k + 1, :], (n, n)).T[:, :1]


def places(routes, experts, capacity):
    tokens = routes.shape[1]
    lane = lax.broadcasted_iota(jnp.int32, (tokens, experts), 1)
    chosen = [column(routes.astype(F32), k).astype(jnp.int32) for k in range(2)]
    hot = [(c == lane).astype(F32) for c in chosen]
    earlier = (
        lax.broadcasted_iota(jnp.int32, (tokens, tokens), 1)
        < lax.broadcasted_iota(jnp.int32, (tokens, tokens), 0)
    ).astype(BF16)
    before = [jnp.dot(earlier, h.astype(BF16), preferred_element_type=F32) for h in hot]
    before[1] = before[1] + jnp.sum(hot[0], axis=0, keepdims=True)
    slot = lax.broadcasted_iota(jnp.int32, (tokens, experts * capacity), 1)
    found = []
    for k in range(2):
        position = jnp.sum(before[k] * hot[k], axis=1, keepdims=True).astype(jnp.int32)
        found.append((slot == chosen[k] * capacity + position).astype(BF16))
    return found


def turned_dot(a, b):
    return lax.dot_general(a, b, (((0,), (0,)), ((), ())), preferred_element_type=F32)


def pack_body(experts, capacity, *refs):
    packed, scratch = refs[-2:]
    sets = len(refs) // 2 - 1
    deep = packed.shape[1] // sets
    for i in range(sets):
        latent, routes = refs[2 * i : 2 * i + 2]
        wide = latent[...].astype(F32)
        scale = lax.rsqrt(jnp.mean(wide * wide, axis=1, keepdims=True) + 1e-06)
        normed = (wide * scale).astype(BF16)
        first, second = places(routes[...], experts, capacity)
        store_flat(turned_dot(first + second, normed), scratch)
        packed[:, i * deep : (i + 1) * deep, :] = (
            scratch[...].reshape(experts, deep, LANES).astype(BF16)
        )


def forward_body(flat, gate, up, down, gate2, up2, down2, rows, partial, scratch, total):
    j = pl.program_id(0)
    pieces = rows.shape[1] // LANES

    @pl.when(j == 0)
    def _():
        scratch[...] = flat[...].astype(F32).reshape(scratch.shape)
        for c in range(pieces):
            rows[:, c * LANES : (c + 1) * LANES] = load_flat(scratch, pieces, c).astype(BF16)

    x = rows[...]
    found = None
    for g, u, d in ((gate, up, down), (gate2, up2, down2)):
        pre_gate = jnp.dot(x, g[0], preferred_element_type=F32)
        pre_up = jnp.dot(x, u[0], preferred_element_type=F32)
        hidden = (jax.nn.silu(pre_gate) * pre_up).astype(BF16)
        part = jnp.dot(hidden, d[0], preferred_element_type=F32)
        found = part if found is None else found + part

    @pl.when(j == 0)
    def _():
        total[...] = found

    @pl.when(j == pl.num_programs(0) - 1)
    def _():
        store_flat(total[...] + found, scratch)
        partial[...] = scratch[...].reshape(partial.shape).astype(partial.dtype)


def forward(flat, part, parts, mine, other, width, dtype):
    steps = 2
    experts, deep = flat.shape[0], flat.shape[1] // parts
    count = experts * deep * LANES // width
    hidden = mine[0].shape[2]
    cut = hidden // steps
    across = pl.BlockSpec((1, width, cut), lambda j: (0, 0, j))
    down = pl.BlockSpec((1, cut, width), lambda j: (0, j, 0))
    return call(
        forward_body,
        (
            jax.ShapeDtypeStruct((count, width), BF16),
            jax.ShapeDtypeStruct((experts, deep, LANES), dtype),
        ),
        (pltpu.VMEM((experts * deep, LANES), F32), pltpu.VMEM((count, width), F32)),
        mib=62,
        cost=12 * count * width * hidden,
        grid=(steps,),
        in_specs=[
            pl.BlockSpec((experts, deep, LANES), lambda j: (0, part, 0)),
            across, across, down, across, across, down,
        ],
        out_specs=(
            pl.BlockSpec((count, width), lambda j: (0, 0)),
            pl.BlockSpec((experts, deep, LANES), lambda j: (0, 0, 0)),
        ),
    )(flat, *mine, *other)


def factors_body(rows, gate, up, turned_rows, turned_hidden, by_gate, by_up):
    x = rows[...]
    pre_gate = jnp.dot(x, gate[0], preferred_element_type=F32)
    pre_up = jnp.dot(x, up[0], preferred_element_type=F32)
    s = jax.nn.sigmoid(pre_gate)
    through = pre_gate * s
    by_gate[...] = pre_up * s * (1.0 + pre_gate * (1.0 - s))
    by_up[...] = through
    turned_hidden[...] = (through * pre_up).astype(BF16).T
    turned_rows[...] = x.T


def factors(rows, gate, up):
    count, width = rows.shape
    hidden = gate.shape[2]
    cut = 256
    held = pl.BlockSpec((1, width, hidden), lambda i: (0, 0, 0))
    return call(
        factors_body,
        (
            jax.ShapeDtypeStruct((width, count), BF16),
            jax.ShapeDtypeStruct((hidden, count), BF16),
            jax.ShapeDtypeStruct((count, hidden), F32),
            jax.ShapeDtypeStruct((count, hidden), F32),
        ),
        mib=62,
        cost=4 * count * width * hidden,
        grid=(count // cut,),
        in_specs=[pl.BlockSpec((cut, width), lambda i: (i, 0)), held, held],
        out_specs=(
            pl.BlockSpec((width, cut), lambda i: (0, i)),
            pl.BlockSpec((hidden, cut), lambda i: (0, i)),
            pl.BlockSpec((cut, hidden), lambda i: (i, 0)),
            pl.BlockSpec((cut, hidden), lambda i: (i, 0)),
        ),
    )(rows, gate, up)


def combine_body(
    experts, capacity, factor, s_flat, t_flat, s_latent, t_latent, s_routes, t_routes, s_mixing,
    t_mixing, packed, scratch, gathered,
):
    pieces = s_latent.shape[1] // LANES
    found = []
    for flat, latent, routes, mixing in (
        (s_flat, s_latent, s_routes, s_mixing),
        (t_flat, t_latent, t_routes, t_mixing),
    ):
        scratch[...] = flat[...].astype(F32).reshape(scratch.shape)
        for c in range(pieces):
            gathered[:, c * LANES : (c + 1) * LANES] = load_flat(scratch, pieces, c).astype(BF16)
        where = places(routes[...], experts, capacity)
        mixed = [column(mixing[...], k) for k in range(2)]
        picked = [
            jnp.dot(w, gathered[...], preferred_element_type=F32) * mixed[k]
            for k, w in enumerate(where)
        ]
        found.append((latent[...].astype(F32) + (picked[0] + picked[1]), where, mixed))
    cotangent = factor * (found[0][0] - found[1][0])
    where, mixed = found[0][1:]
    slots = [
        turned_dot(w, (mixed[k] * cotangent).astype(BF16)) for k, w in enumerate(where)
    ]
    store_flat(slots[0] + slots[1], scratch)
    packed[...] = scratch[...].reshape(packed.shape).astype(BF16)


def backward_body(last, *refs):
    one, two, down, turned_rows, turned_hidden, by_gate, by_up = refs[:7]
    earlier = refs[7:10] if last else (None,) * 3
    gate_out, up_out, down_out, scratch, cotangent = refs[-5:]
    pieces = down.shape[2] // LANES

    @pl.when(pl.program_id(0) == 0)
    def _():
        count = cotangent.shape[0] // 2
        for b, flat in enumerate((one, two)):
            scratch[...] = flat[...].astype(F32).reshape(scratch.shape)
            for c in range(pieces):
                cotangent[b * count : (b + 1) * count, c * LANES : (c + 1) * LANES] = load_flat(
                    scratch, pieces, c
                ).astype(BF16)

    back = cotangent[...]
    grad_hidden = lax.dot_general(
        back, down[0], (((1,), (1,)), ((), ())), preferred_element_type=F32
    )
    grad_gate = (grad_hidden * by_gate[...]).astype(BF16)
    grad_up = (grad_hidden * by_up[...]).astype(BF16)
    for out, before, left, right in (
        (gate_out, earlier[0], turned_rows, grad_gate),
        (up_out, earlier[1], turned_rows, grad_up),
        (down_out, earlier[2], turned_hidden, back),
    ):
        found = jnp.dot(left[...], right, preferred_element_type=F32)
        out[0] = (found if before is None else found + before[0]).astype(out.dtype)


def backward(blocks, turn, down, turned_rows, turned_hidden, by_gate, by_up, earlier=()):
    steps = 2
    hidden, width = down.shape[1:]
    count = turned_rows.shape[1] // 2
    cut = hidden // steps
    dtype = BF16 if earlier else F32
    flat = pl.BlockSpec(blocks[0].shape, lambda j: (0, 0, 0))
    flat_rows = blocks[0].shape[0] * blocks[0].shape[1]
    grads = [
        pl.BlockSpec((1, width, cut), lambda j: (0, 0, j)),
        pl.BlockSpec((1, width, cut), lambda j: (0, 0, j)),
        pl.BlockSpec((1, cut, width), lambda j: (0, j, 0)),
    ]
    return call(
        functools.partial(backward_body, bool(earlier)),
        (
            jax.ShapeDtypeStruct((1, width, hidden), dtype),
            jax.ShapeDtypeStruct((1, width, hidden), dtype),
            jax.ShapeDtypeStruct((1, hidden, width), dtype),
        ),
        (pltpu.VMEM((flat_rows, LANES), F32), pltpu.VMEM((count, width), BF16)),
        cost=4 * count * 2 * width * hidden,
        grid=(steps,),
        in_specs=[
            flat, flat,
            pl.BlockSpec((1, cut, width), lambda j: (0, j, 0)),
            pl.BlockSpec((width, count), lambda j: (0, turn)),
            pl.BlockSpec((cut, count), lambda j: (j, turn)),
            pl.BlockSpec((count, cut), lambda j: (turn, j)),
            pl.BlockSpec((count, cut), lambda j: (turn, j)),
            *(grads if earlier else ()),
        ],
        out_specs=tuple(grads),
    )(*blocks, down, turned_rows, turned_hidden, by_gate, by_up, *earlier)


def to_experts(blocks):
    return lax.all_to_all(blocks, "expert", split_axis=0, concat_axis=0, tiled=True)


def other_core(value):
    return lax.ppermute(value, "dp", ((0, 1), (1, 0), (2, 3), (3, 2)))


def other_chip(value):
    return lax.ppermute(value, "dp", ((0, 2), (2, 0), (1, 3), (3, 1)))


def shards(
    student_latent,
    target_latent,
    student_gate,
    student_up,
    student_down,
    target_gate,
    target_up,
    target_down,
    student_routes,
    target_routes,
    student_mixing,
    target_mixing,
):
    groups = lax.axis_size("dp")
    experts = lax.axis_size("expert")
    tokens, width = student_latent.shape
    top = student_routes.shape[1]
    capacity = tokens * top * 5 // (4 * experts)
    slots = experts * capacity
    deep = capacity * width // LANES
    flat_shape = (experts * deep, LANES)
    blocks_shape = (experts, deep, LANES)

    def packing(*sets):
        return call(
            functools.partial(pack_body, experts, capacity),
            jax.ShapeDtypeStruct((experts, len(sets) // 2 * deep, LANES), BF16),
            (pltpu.VMEM(flat_shape, F32),),
            mib=12,
            cost=2 * tokens * slots * width,
        )(*sets)

    student_routes, target_routes = student_routes.T, target_routes.T
    student_mixing, target_mixing = student_mixing.T, target_mixing.T
    far_latent = other_chip(target_latent)
    far_routes = other_chip(target_routes)
    sent_student = packing(student_latent, student_routes)
    sent_target = packing(target_latent, target_routes, far_latent, far_routes)
    own_student = to_experts(sent_student)
    both_target = to_experts(sent_target)
    student = (student_gate, student_up, student_down)
    target = (target_gate, target_up, target_down)
    student2 = tuple(other_core(w) for w in student)
    target2 = tuple(other_core(w) for w in target)
    far_student = other_chip(own_student)

    own_rows, own_part = forward(own_student, 0, 1, student, student2, width, F32)
    far_rows, far_part = forward(far_student, 0, 1, student, student2, width, BF16)
    own_part_t = forward(both_target, 0, 2, target, target2, width, F32)[1]
    far_part_t = forward(both_target, 1, 2, target, target2, width, BF16)[1]
    came_s = other_chip(far_part)
    came_t = other_chip(far_part_t)
    student_sum = (own_part + came_s.astype(F32)).astype(BF16)
    target_sum = (own_part_t + came_t.astype(F32)).astype(BF16)
    back_student = to_experts(student_sum)
    back_target = to_experts(target_sum)

    rows = jnp.concatenate([own_rows, other_core(own_rows), far_rows, other_core(far_rows)], axis=0)
    turned_rows, turned_hidden, by_gate, by_up = factors(rows, student_gate, student_up)

    factor = (experts / (top * tokens * groups * experts)) ** 0.5
    slot_values = call(
        functools.partial(combine_body, experts, capacity, factor),
        jax.ShapeDtypeStruct(blocks_shape, BF16),
        (pltpu.VMEM(flat_shape, F32), pltpu.VMEM((slots, width), BF16)),
        mib=16,
        cost=8 * tokens * slots * width,
    )(
        back_student, back_target, student_latent, target_latent, student_routes,
        target_routes, student_mixing, target_mixing,
    )
    own_cot = to_experts(slot_values)
    far_cot = other_chip(own_cot)
    own_cot2 = other_core(own_cot)
    given = (student_down, turned_rows, turned_hidden, by_gate, by_up)
    near = backward((own_cot, own_cot2), 0, *given)
    far_cot2 = other_core(far_cot)
    return backward((far_cot, far_cot2), 1, *given, tuple(near))


def solution(mesh):
    in_specs = (
        P(("dp", "expert"), None),
        P(("dp", "expert"), None),
        P("expert", None, "dp"),
        P("expert", None, "dp"),
        P("expert", "dp", None),
        P("expert", None, "dp"),
        P("expert", None, "dp"),
        P("expert", "dp", None),
        P(("dp", "expert"), None),
        P(("dp", "expert"), None),
        P(("dp", "expert"), None),
        P(("dp", "expert"), None),
    )
    out_specs = (P("expert", None, "dp"), P("expert", None, "dp"), P("expert", "dp", None))
    return jax.shard_map(shards, mesh=mesh, in_specs=in_specs, out_specs=out_specs, check_vma=False)
```

time: 386 us -> 250 us (0.65)
  waiting for transfers between devices: 216 us -> 59.7 us
  Pallas kernels: 0 us -> 58.1 us
  matrix products: 36.1 us -> 0 us
  starting transfers between devices: 41.5 us -> 64.5 us
  local copies, waits for them, and re-layouts: 32.4 us -> 10.8 us
  blocking collectives: 32.6 us -> 50.1 us
  between operations: 14.4 us -> 0.86 us
  other arithmetic: 11.8 us -> 5.42 us
    all_gather x2 -> x0, waiting for transfers between devices: 81.1 us -> none  [the longest x1 48.2 us: sent_together(): lax.all_gather(both, axis, axis=dim, tiled=True)]
    reduce_scatter x2 -> x0, waiting for transfers between devices: 70 us -> none  [the longest x1 39.1 us: return_pair(): lax.psum_scatter(student_sum.astype(jnp.bfloat16), 'dp', scatter_dimensio...]
    all_to_all x4 -> x3, waiting for transfers between devices: 65.3 us -> 1.2 us  [to_experts(): lax.all_to_all(blocks, 'expert', split_axis=0, concat_axis=0, tiled=True)]
    ppermute x0 -> x16, waiting for transfers between devices: none -> 58.5 us  [the longest x6 55.8 us: other_chip(): return lax.ppermute(value, 'dp', ((0, 2), (2, 0), (1, 3), (3, 1)))]
    pallas_call x0 -> x10, Pallas kernels: none -> 58.1 us  [the longest x4 27 us: forward(): call(forward_body, (jax.ShapeDtypeStruct((count, width), BF16), jax.Shape...]
    dot_general x9 -> x0, matrix products: 36.1 us -> none  [the longest x2 10.7 us: expert_forward(): jnp.dot(hidden, weight_down, preferred_element_type=jnp.float32)]
    ppermute x0 -> x16, starting transfers between devices: none -> 28.3 us  [the longest x10 15.4 us: other_core(): return lax.ppermute(value, 'dp', ((0, 1), (1, 0), (2, 3), (3, 2)))]
    all_to_all x1 -> x2, blocking collectives: 32.6 us -> 50.1 us  [to_experts(): lax.all_to_all(blocks, 'expert', split_axis=0, concat_axis=0, tiled=True)]
  transfers between devices with their start and end apart: 8 -> 19, of which waited for: 7 -> 8; matrix products, arithmetic and copies ran while one was open for 5% -> 2% of each run, Pallas kernels for 0% -> 18%
where the time goes in v1:
time: 250 us; the launch traced here: 249 us
  starting transfers between devices  64.5 us (26%)
  waiting for transfers between devices  59.7 us (24%)
  Pallas kernels  58.1 us (23%)
  blocking collectives  50.1 us (20%)
  local copies, waits for them, and re-layouts  10.8 us (4%)
  other arithmetic  5.42 us (2%)
    ppermute x6, waiting for transfers between devices, other_chip(): return lax.ppermute(value, 'dp', ((0, 2), (2, 0), (1, 3), (3, 1)))  55.8 us
    all_to_all x2, blocking collectives, to_experts(): lax.all_to_all(blocks, 'expert', split_axis=0, concat_axis=0, tiled=True)  50.1 us
    all_to_all x3, starting transfers between devices, to_experts(): lax.all_to_all(blocks, 'expert', split_axis=0, concat_axis=0, tiled=True)  36.1 us
    pallas_call x4, Pallas kernels, forward(): call(forward_body, (jax.ShapeDtypeStruct((count, width), BF16), jax.Shape...  27 us
    pallas_call x2, Pallas kernels, backward(): call(functools.partial(backward_body, bool(earlier)), (jax.ShapeDtypeStru...  15.5 us
    ppermute x10, starting transfers between devices, other_core(): return lax.ppermute(value, 'dp', ((0, 1), (1, 0), (2, 3), (3, 2)))  15.4 us
    ppermute x6, starting transfers between devices, other_chip(): return lax.ppermute(value, 'dp', ((0, 2), (2, 0), (1, 3), (3, 1)))  13 us
    unnamed x46, local copies, waits for them, and re-layouts  10.8 us
  transfers between devices with their start and end apart: 19, of which 8 were waited for; matrix products, arithmetic and copies ran while one was open for 2% of the time, Pallas kernels for 18%

profile of v1, /device:TPU:1, one launch (start us, length us, event | category | flops | bytes accessed | tf_op | source)
XLA Modules:
  0.0 249.3 jit_solution(6895210307755532875)
XLA Ops:
  2.3 1.8 shard_map.139
  4.0 13.6 %all-to-all-start = ((bf16[64,40,128]{2,1,0:T(8,128)(2,1)}), bf16[64,40,128]{2,1,0:T(8,128)(2,1)S(1)}, u32[]{:S(2)}, u32[]{:S(2)}) async-start(bf16[64,40,128]{2,1,0:T(8,128)(2,1)} %shard_map.139), calls=%async_computation | async-start | bytes 1310720 | tf_op jit(solution)/shard_map/all_to_all | solution.py:278
  17.7 2.7 %collective-permute-start.5 = (bf16[128,1024]{1,0:T(8,128)(2,1)}, bf16[128,1024]{1,0:T(8,128)(2,1)S(1)}, u32[]{:S(2)}, u32[]{:S(2)}) collective-permute-start(bf16[128,1024]{1,0:T(8,128)(2,1)} %t_latent.1), channel_id=1, source_target_pairs={{0,128},{128,0},{64,192},{192,64},{1,129},{129,1},{65,193},{193,65... | collective-permute-start | bytes 786440 | tf_op jit(solution)/shard_map/ppermute | solution.py:286
  20.7 9.3 %collective-permute-done.6.refs_3_ = s32[2,128]{1,0:T(2,128)S(1)} collective-permute-done((s32[2,128]{1,0:T(2,128)}, s32[2,128]{1,0:T(2,128)S(1)}, u32[]{:S(2)}, u32[]{:S(2)}) %collective-permute-start.6) | collective-permute-done | bytes 1056 | tf_op jit(solution)/shard_map/ppermute | solution.py:286
  31.6 2.7 %shard_map.142 = bf16[64,80,128]{2,1,0:T(8,128)(2,1)} custom-call(bf16[128,1024]{1,0:T(8,128)(2,1)S(1)} %copy-done.8, s32[2,128]{1,0:T(2,128)S(1)} %bitcast.5, bf16[128,1024]{1,0:T(8,128)(2,1)S(1)} %collective-permute-done.5.refs_2_, s32[2,128]{1,0:T(2,128)S(1)} %collective-permute-done.6.refs_3_), custom_call_target="tpu_custom_call" | custom-call | flops 83886080 | bytes 1048576 | tf_op jit(solution)/shard_map/pallas_call | solution.py:314
  35.5 12.2 %all-to-all-start.2 = ((bf16[64,80,128]{2,1,0:T(8,128)(2,1)}), bf16[64,80,128]{2,1,0:T(8,128)(2,1)}, u32[]{:S(2)}, u32[]{:S(2)}) async-start(bf16[64,80,128]{2,1,0:T(8,128)(2,1)} %shard_map.142), calls=%async_computation.2 | async-start | bytes 2621440 | tf_op jit(solution)/shard_map/all_to_all | solution.py:278
  49.8 2.4 collective-permute-start.3
  55.8 23.5 %collective-permute-done.3.flat = bf16[64,40,128]{2,1,0:T(8,128)(2,1)} collective-permute-done((bf16[64,40,128]{2,1,0:T(8,128)(2,1)S(1)}, bf16[64,40,128]{2,1,0:T(8,128)(2,1)}, u32[]{:S(2)}, u32[]{:S(2)}) %collective-permute-start.3) | collective-permute-done | bytes 655392 | tf_op jit(solution)/shard_map/ppermute | solution.py:286
  79.3 6.9 %shard_map.141 = (bf16[320,1024]{1,0:T(8,128)(2,1)}, bf16[64,40,128]{2,1,0:T(8,128)(2,1)}) custom-call(bf16[64,40,128]{2,1,0:T(8,128)(2,1)} %collective-permute-done.3.flat, bf16[1,1024,512]{2,1,0:T(8,128)(2,1)} %gate.9, bf16[1,1024,512]{2,1,0:T(8,128)(2,1)} %up.9, bf16[1,512,1024]{2,1,0:T(8,128)(2,1)} %refs_2_.3, bf16[1,1024,512]{2,1,0:T(8,128)(2,1)} %copy-done.20, ...), custom_call_target="tpu_custom_call" | custom-call | flops 2013265920 | bytes 1048576 | tf_op jit(solution)/shard_map/pallas_call | solution.py:122
  86.2 2.5 %collective-permute-start.4 = (bf16[64,40,128]{2,1,0:T(8,128)(2,1)}, bf16[64,40,128]{2,1,0:T(8,128)(2,1)S(1)}, u32[]{:S(2)}, u32[]{:S(2)}) collective-permute-start(bf16[64,40,128]{2,1,0:T(8,128)(2,1)} %get-tuple-element.17), channel_id=1, source_target_pairs={{0,128},{128,0},{64,192},{192,64},{1,129},{129,1},{65,193},{193,65... | collective-permute-start | bytes 1966088 | tf_op jit(solution)/shard_map/ppermute | solution.py:286
  89.9 7.1 %shard_map.140 = (bf16[320,1024]{1,0:T(8,128)(2,1)}, f32[64,40,128]{2,1,0:T(8,128)}) custom-call(bf16[64,40,128]{2,1,0:T(8,128)(2,1)} %copy-done.19, bf16[1,1024,512]{2,1,0:T(8,128)(2,1)} %gate.9, bf16[1,1024,512]{2,1,0:T(8,128)(2,1)} %up.9, bf16[1,512,1024]{2,1,0:T(8,128)(2,1)} %refs_2_.3, bf16[1,1024,512]{2,1,0:T(8,128)(2,1)} %copy-done.20, ...), custom_call_target="tpu_custom_call" | custom-call | flops 2013265920 | bytes 1048576 | tf_op jit(solution)/shard_map/pallas_call | solution.py:122
  97.0 6.4 %collective-permute-done.4 = bf16[64,40,128]{2,1,0:T(8,128)(2,1)S(1)} collective-permute-done((bf16[64,40,128]{2,1,0:T(8,128)(2,1)}, bf16[64,40,128]{2,1,0:T(8,128)(2,1)S(1)}, u32[]{:S(2)}, u32[]{:S(2)}) %collective-permute-start.4) | collective-permute-done | bytes 655392 | tf_op jit(solution)/shard_map/ppermute | solution.py:286
  103.5 2.3 add_convert_fusion.1
  105.7 10.3 %all-to-all-start.1 = ((bf16[64,40,128]{2,1,0:T(8,128)(2,1)}), bf16[64,40,128]{2,1,0:T(8,128)(2,1)S(1)}, u32[]{:S(2)}, u32[]{:S(2)}) async-start(bf16[64,40,128]{2,1,0:T(8,128)(2,1)} %add_convert_fusion.1), calls=%async_computation.1 | async-start | bytes 1310720 | tf_op jit(solution)/shard_map/all_to_all | solution.py:278
  116.1 6.4 %shard_map.144 = (bf16[320,1024]{1,0:T(8,128)(2,1)}, bf16[64,40,128]{2,1,0:T(8,128)(2,1)}) custom-call(bf16[64,80,128]{2,1,0:T(8,128)(2,1)} %all-to-all-done.2.flat, bf16[1,1024,512]{2,1,0:T(8,128)(2,1)} %gate.8, bf16[1,1024,512]{2,1,0:T(8,128)(2,1)} %up.8, bf16[1,512,1024]{2,1,0:T(8,128)(2,1)} %down.7, bf16[1,1024,512]{2,1,0:T(8,128)(2,1)} %collective-permute-done.7.gate2, ...), custom_call_target="tpu_custom_call" | custom-call | flops 2013265920 | bytes 1048576 | tf_op jit(solution)/shard_map/pallas_call | solution.py:122
  122.5 2.6 %collective-permute-start.10 = (bf16[64,40,128]{2,1,0:T(8,128)(2,1)}, bf16[64,40,128]{2,1,0:T(8,128)(2,1)S(1)}, u32[]{:S(2)}, u32[]{:S(2)}) collective-permute-start(bf16[64,40,128]{2,1,0:T(8,128)(2,1)} %get-tuple-element.19), channel_id=1, source_target_pairs={{0,128},{128,0},{64,192},{192,64},{1,129},{129,1},{65,193},{193,65... | collective-permute-start | bytes 1966088 | tf_op jit(solution)/shard_map/ppermute | solution.py:286
  125.1 6.6 %shard_map.143 = (bf16[320,1024]{1,0:T(8,128)(2,1)}, f32[64,40,128]{2,1,0:T(8,128)}) custom-call(bf16[64,80,128]{2,1,0:T(8,128)(2,1)} %all-to-all-done.2.flat, bf16[1,1024,512]{2,1,0:T(8,128)(2,1)} %gate.8, bf16[1,1024,512]{2,1,0:T(8,128)(2,1)} %up.8, bf16[1,512,1024]{2,1,0:T(8,128)(2,1)} %down.7, bf16[1,1024,512]{2,1,0:T(8,128)(2,1)} %collective-permute-done.7.gate2, ...), custom_call_target="tpu_custom_call" | custom-call | flops 2013265920 | bytes 1048576 | tf_op jit(solution)/shard_map/pallas_call | solution.py:122
  131.8 12.1 %collective-permute-done.10 = bf16[64,40,128]{2,1,0:T(8,128)(2,1)S(1)} collective-permute-done((bf16[64,40,128]{2,1,0:T(8,128)(2,1)}, bf16[64,40,128]{2,1,0:T(8,128)(2,1)S(1)}, u32[]{:S(2)}, u32[]{:S(2)}) %collective-permute-start.10) | collective-permute-done | bytes 655392 | tf_op jit(solution)/shard_map/ppermute | solution.py:286
  145.3 25.9 %all_to_all.25.t_flat = bf16[64,40,128]{2,1,0:T(8,128)(2,1)S(1)} all-to-all(bf16[64,40,128]{2,1,0:T(8,128)(2,1)S(1)} %add_convert_fusion), channel_id=1, replica_groups=mesh['dp'=4,'expert'=64] {'expert'}, dimensions={0} | all-to-all | bytes 1310720 | tf_op jit(solution)/shard_map/all_to_all | solution.py:278
  171.2 2.7 %shard_map.145 = bf16[64,40,128]{2,1,0:T(8,128)(2,1)S(1)} custom-call(bf16[64,40,128]{2,1,0:T(8,128)(2,1)S(1)} %all-to-all-done.1.s_flat, bf16[64,40,128]{2,1,0:T(8,128)(2,1)S(1)} %all_to_all.25.t_flat, bf16[128,1024]{1,0:T(8,128)(2,1)S(1)} %copy-done.7, bf16[128,1024]{1,0:T(8,128)(2,1)S(1)} %copy-done.9, s32[2,128]{1,0:T(2,128)S(1)} %bitcast.8, ...), custom_call_target="tpu_custom_call" | custom-call | flops 335544320 | bytes 1048576 | tf_op jit(solution)/shard_map/pallas_call | solution.py:351
  173.9 24.1 %all_to_all.26.refs_0_ = bf16[64,40,128]{2,1,0:T(8,128)(2,1)S(1)} all-to-all(bf16[64,40,128]{2,1,0:T(8,128)(2,1)S(1)} %shard_map.145), channel_id=1, replica_groups=mesh['dp'=4,'expert'=64] {'expert'}, dimensions={0} | all-to-all | bytes 1310720 | tf_op jit(solution)/shard_map/all_to_all | solution.py:278
  198.1 2.5 collective-permute-start.11
  200.5 5.6 %collective-permute-start.13 = (bf16[320,1024]{1,0:T(8,128)(2,1)S(1)}, bf16[320,1024]{1,0:T(8,128)(2,1)S(1)}, u32[]{:S(2)}, u32[]{:S(2)}) collective-permute-start(bf16[320,1024]{1,0:T(8,128)(2,1)S(1)} %copy-done.18), channel_id=1, source_target_pairs={{0,64},{64,0},{128,192},{192,128},{1,65},{65,1},{129,193},{193,129... | collective-permute-start | bytes 1966088 | tf_op jit(solution)/shard_map/ppermute | solution.py:282
  206.7 4.6 %collective-permute-done.11.refs_0_ = bf16[64,40,128]{2,1,0:T(8,128)(2,1)} collective-permute-done((bf16[64,40,128]{2,1,0:T(8,128)(2,1)S(1)}, bf16[64,40,128]{2,1,0:T(8,128)(2,1)}, u32[]{:S(2)}, u32[]{:S(2)}) %collective-permute-start.11) | collective-permute-done | bytes 655392 | tf_op jit(solution)/shard_map/ppermute | solution.py:286
  211.3 5.9 %collective-permute-start.12 = (bf16[64,40,128]{2,1,0:T(8,128)(2,1)}, bf16[64,40,128]{2,1,0:T(8,128)(2,1)}, u32[]{:S(2)}, u32[]{:S(2)}) collective-permute-start(bf16[64,40,128]{2,1,0:T(8,128)(2,1)} %collective-permute-done.11.refs_0_), channel_id=1, source_target_pairs={{0,64},{64,0},{128,192},{192,128},{1,65},{65,1},{129,193},{193,129... | collective-permute-start | bytes 1966088 | tf_op jit(solution)/shard_map/ppermute | solution.py:282
  217.2 1.7 pad_maximum_fusion.rows
  218.9 8.4 %shard_map.146 = (bf16[1024,1280]{1,0:T(8,128)(2,1)}, bf16[512,1280]{1,0:T(8,128)(2,1)}, f32[1280,512]{1,0:T(8,128)}, f32[1280,512]{1,0:T(8,128)}) custom-call(bf16[1280,1024]{1,0:T(8,128)(2,1)} %pad_maximum_fusion.rows, bf16[1,1024,512]{2,1,0:T(8,128)(2,1)} %gate.9, bf16[1,1024,512]{2,1,0:T(8,128)(2,1)} %up.9), custom_call_target="tpu_custom_call" | custom-call | flops 2684354560 | bytes 1048576 | tf_op jit(solution)/shard_map/pallas_call | solution.py:160
  227.3 1.7 copy-done
  229.0 1.7 copy-done.1
  230.8 1.7 copy-done.2
  233.8 7.3 %shard_map.147 = (f32[1,1024,512]{2,1,0:T(8,128)S(1)}, f32[1,1024,512]{2,1,0:T(8,128)S(1)}, f32[1,512,1024]{2,1,0:T(8,128)S(1)}) custom-call(bf16[64,40,128]{2,1,0:T(8,128)(2,1)S(1)} %all_to_all.26.refs_0_, bf16[64,40,128]{2,1,0:T(8,128)(2,1)} %collective-permute-done.15.refs_1_, bf16[1,512,1024]{2,1,0:T(8,128)(2,1)S(1)} %copy-done.5, ...), custom_call_target="tpu_custom_call" | custom-call | flops 2684354560 | bytes 1048576 | tf_op jit(solution)/shard_map/pallas_call | solution.py:254
  241.1 8.2 %shard_map.148 = (bf16[1,1024,512]{2,1,0:T(8,128)(2,1)}, bf16[1,1024,512]{2,1,0:T(8,128)(2,1)}, bf16[1,512,1024]{2,1,0:T(8,128)(2,1)}) custom-call(bf16[64,40,128]{2,1,0:T(8,128)(2,1)} %collective-permute-done.11.refs_0_, bf16[64,40,128]{2,1,0:T(8,128)(2,1)} %collective-permute-done.12.refs_1_, bf16[1,512,1024]{2,1,0:T(8,128)(2,1)S(1)} %copy-done.5, ...), custom_call_target="tpu_custom_call" | custom-call | flops 2684354560 | bytes 1048576 | tf_op jit(solution)/shard_map/pallas_call | solution.py:254
  (67 shorter events, 15.1 us)
Async XLA Ops:
  4.0 45.4 %copy-start.4 = (bf16[1,512,1024]{2,1,0:T(8,128)(2,1)S(1)}, bf16[1,512,1024]{2,1,0:T(8,128)(2,1)}, u32[]{:S(2)}) copy-start(bf16[1,512,1024]{2,1,0:T(8,128)(2,1)} %refs_2_.3) | copy-start | bytes 3145732
  4.0 31.5 %all-to-all-start = ((bf16[64,40,128]{2,1,0:T(8,128)(2,1)}), bf16[64,40,128]{2,1,0:T(8,128)(2,1)S(1)}, u32[]{:S(2)}, u32[]{:S(2)}) async-start(bf16[64,40,128]{2,1,0:T(8,128)(2,1)} %shard_map.139), calls=%async_computation | async-start | bytes 1310720 | tf_op jit(solution)/shard_map/all_to_all | solution.py:278
  17.7 12.4 %collective-permute-start.5 = (bf16[128,1024]{1,0:T(8,128)(2,1)}, bf16[128,1024]{1,0:T(8,128)(2,1)S(1)}, u32[]{:S(2)}, u32[]{:S(2)}) collective-permute-start(bf16[128,1024]{1,0:T(8,128)(2,1)} %t_latent.1), channel_id=1, source_target_pairs={{0,128},{128,0},{64,192},{192,64},{1,129},{129,1},{65,193},{193,65... | collective-permute-start | bytes 786440 | tf_op jit(solution)/shard_map/ppermute | solution.py:286
  20.4 9.6 %collective-permute-start.6 = (s32[2,128]{1,0:T(2,128)}, s32[2,128]{1,0:T(2,128)S(1)}, u32[]{:S(2)}, u32[]{:S(2)}) collective-permute-start(s32[2,128]{1,0:T(2,128)} %bitcast.4), channel_id=1, source_target_pairs={{0,128},{128,0},{64,192},{192,64},{1,129},{129,1},{65,193},{193,65... | collective-permute-start | bytes 3080 | tf_op jit(solution)/shard_map/ppermute | solution.py:286
  35.5 50.6 %copy-start.19 = (bf16[64,40,128]{2,1,0:T(8,128)(2,1)}, bf16[64,40,128]{2,1,0:T(8,128)(2,1)S(1)}, u32[]{:S(2)}) copy-start(bf16[64,40,128]{2,1,0:T(8,128)(2,1)S(1)} %all-to-all-done.flat) | copy-start | bytes 1966084
  35.5 70.2 %all-to-all-start.2 = ((bf16[64,80,128]{2,1,0:T(8,128)(2,1)}), bf16[64,80,128]{2,1,0:T(8,128)(2,1)}, u32[]{:S(2)}, u32[]{:S(2)}) async-start(bf16[64,80,128]{2,1,0:T(8,128)(2,1)} %shard_map.142), calls=%async_computation.2 | async-start | bytes 2621440 | tf_op jit(solution)/shard_map/all_to_all | solution.py:278
  47.7 41.0 %copy-start.16 = (bf16[1,1024,512]{2,1,0:T(8,128)(2,1)S(1)}, bf16[1,1024,512]{2,1,0:T(8,128)(2,1)}, u32[]{:S(2)}) copy-start(bf16[1,1024,512]{2,1,0:T(8,128)(2,1)} %gate.8) | copy-start | bytes 3145732
  47.7 4.5 %collective-permute-start = (bf16[1,1024,512]{2,1,0:T(8,128)(2,1)}, bf16[1,1024,512]{2,1,0:T(8,128)(2,1)S(1)}, u32[]{:S(2)}, u32[]{:S(2)}) collective-permute-start(bf16[1,1024,512]{2,1,0:T(8,128)(2,1)} %gate.9), channel_id=1, source_target_pairs={{0,64},{64,0},{128,192},{192,128},{1,65},{65,1},{129,193},{193,129... | collective-permute-start | bytes 3145736 | tf_op jit(solution)/shard_map/ppermute | solution.py:282
  49.3 4.0 %collective-permute-start.1 = (bf16[1,1024,512]{2,1,0:T(8,128)(2,1)}, bf16[1,1024,512]{2,1,0:T(8,128)(2,1)S(1)}, u32[]{:S(2)}, u32[]{:S(2)}) collective-permute-start(bf16[1,1024,512]{2,1,0:T(8,128)(2,1)} %up.9), channel_id=1, source_target_pairs={{0,64},{64,0},{128,192},{192,128},{1,65},{65,1},{129,193},{193,129... | collective-permute-start | bytes 3145736 | tf_op jit(solution)/shard_map/ppermute | solution.py:282
  49.4 5.4 %collective-permute-start.2 = (bf16[1,512,1024]{2,1,0:T(8,128)(2,1)S(1)}, bf16[1,512,1024]{2,1,0:T(8,128)(2,1)S(1)}, u32[]{:S(2)}, u32[]{:S(2)}) collective-permute-start(bf16[1,512,1024]{2,1,0:T(8,128)(2,1)S(1)} %copy-done.4), channel_id=1, source_target_pairs={{0,64},{64,0},{128,192},{192,128},{1,65},{65,1},{129,193},{193,129... | collective-permute-start | bytes 3145736 | tf_op jit(solution)/shard_map/ppermute | solution.py:282
  49.8 29.5 %collective-permute-start.3 = (bf16[64,40,128]{2,1,0:T(8,128)(2,1)S(1)}, bf16[64,40,128]{2,1,0:T(8,128)(2,1)}, u32[]{:S(2)}, u32[]{:S(2)}) collective-permute-start(bf16[64,40,128]{2,1,0:T(8,128)(2,1)S(1)} %all-to-all-done.flat), channel_id=1, source_target_pairs={{0,128},{128,0},{64,192},{192,64},{1,129},{129,1},{65,193},{193,65... | collective-permute-start | bytes 1966088 | tf_op jit(solution)/shard_map/ppermute | solution.py:286
  52.2 2.6 %copy-start.20 = (bf16[1,1024,512]{2,1,0:T(8,128)(2,1)}, bf16[1,1024,512]{2,1,0:T(8,128)(2,1)S(1)}, u32[]{:S(2)}) copy-start(bf16[1,1024,512]{2,1,0:T(8,128)(2,1)S(1)} %collective-permute-done.gate2) | copy-start | bytes 3145732
  86.2 17.3 %collective-permute-start.4 = (bf16[64,40,128]{2,1,0:T(8,128)(2,1)}, bf16[64,40,128]{2,1,0:T(8,128)(2,1)S(1)}, u32[]{:S(2)}, u32[]{:S(2)}) collective-permute-start(bf16[64,40,128]{2,1,0:T(8,128)(2,1)} %get-tuple-element.17), channel_id=1, source_target_pairs={{0,128},{128,0},{64,192},{192,64},{1,129},{129,1},{65,193},{193,65... | collective-permute-start | bytes 1966088 | tf_op jit(solution)/shard_map/ppermute | solution.py:286
  88.7 27.4 %collective-permute-start.7 = (bf16[1,1024,512]{2,1,0:T(8,128)(2,1)S(1)}, bf16[1,1024,512]{2,1,0:T(8,128)(2,1)}, u32[]{:S(2)}, u32[]{:S(2)}) collective-permute-start(bf16[1,1024,512]{2,1,0:T(8,128)(2,1)S(1)} %copy-done.16), channel_id=1, source_target_pairs={{0,64},{64,0},{128,192},{192,128},{1,65},{65,1},{129,193},{193,129... | collective-permute-start | bytes 3145736 | tf_op jit(solution)/shard_map/ppermute | solution.py:282
  89.4 26.7 %collective-permute-start.8 = (bf16[1,1024,512]{2,1,0:T(8,128)(2,1)}, bf16[1,1024,512]{2,1,0:T(8,128)(2,1)}, u32[]{:S(2)}, u32[]{:S(2)}) collective-permute-start(bf16[1,1024,512]{2,1,0:T(8,128)(2,1)} %up.8), channel_id=1, source_target_pairs={{0,64},{64,0},{128,192},{192,128},{1,65},{65,1},{129,193},{193,129... | collective-permute-start | bytes 3145736 | tf_op jit(solution)/shard_map/ppermute | solution.py:282
  89.4 26.7 %collective-permute-start.9 = (bf16[1,512,1024]{2,1,0:T(8,128)(2,1)}, bf16[1,512,1024]{2,1,0:T(8,128)(2,1)}, u32[]{:S(2)}, u32[]{:S(2)}) collective-permute-start(bf16[1,512,1024]{2,1,0:T(8,128)(2,1)} %down.7), channel_id=1, source_target_pairs={{0,64},{64,0},{128,192},{192,128},{1,65},{65,1},{129,193},{193,129... | collective-permute-start | bytes 3145736 | tf_op jit(solution)/shard_map/ppermute | solution.py:282
  105.7 39.5 %all-to-all-start.1 = ((bf16[64,40,128]{2,1,0:T(8,128)(2,1)}), bf16[64,40,128]{2,1,0:T(8,128)(2,1)S(1)}, u32[]{:S(2)}, u32[]{:S(2)}) async-start(bf16[64,40,128]{2,1,0:T(8,128)(2,1)} %add_convert_fusion.1), calls=%async_computation.1 | async-start | bytes 1310720 | tf_op jit(solution)/shard_map/all_to_all | solution.py:278
  122.5 21.3 %collective-permute-start.10 = (bf16[64,40,128]{2,1,0:T(8,128)(2,1)}, bf16[64,40,128]{2,1,0:T(8,128)(2,1)S(1)}, u32[]{:S(2)}, u32[]{:S(2)}) collective-permute-start(bf16[64,40,128]{2,1,0:T(8,128)(2,1)} %get-tuple-element.19), channel_id=1, source_target_pairs={{0,128},{128,0},{64,192},{192,64},{1,129},{129,1},{65,193},{193,65... | collective-permute-start | bytes 1966088 | tf_op jit(solution)/shard_map/ppermute | solution.py:286
  131.7 39.5 %copy-start.7 = (bf16[128,1024]{1,0:T(8,128)(2,1)S(1)}, bf16[128,1024]{1,0:T(8,128)(2,1)}, u32[]{:S(2)}) copy-start(bf16[128,1024]{1,0:T(8,128)(2,1)} %s_latent.1) | copy-start | bytes 786436
  131.7 39.5 %copy-start.9 = (bf16[128,1024]{1,0:T(8,128)(2,1)S(1)}, bf16[128,1024]{1,0:T(8,128)(2,1)}, u32[]{:S(2)}) copy-start(bf16[128,1024]{1,0:T(8,128)(2,1)} %t_latent.1) | copy-start | bytes 786436
  131.7 39.5 %copy-start.11 = (s32[128,2]{0,1:T(2,128)S(1)}, s32[128,2]{0,1:T(2,128)}, u32[]{:S(2)}) copy-start(s32[128,2]{0,1:T(2,128)} %param.21) | copy-start | bytes 3076
  131.7 39.5 %copy-start.13 = (s32[128,2]{0,1:T(2,128)S(1)}, s32[128,2]{0,1:T(2,128)}, u32[]{:S(2)}) copy-start(s32[128,2]{0,1:T(2,128)} %param.20) | copy-start | bytes 3076
  131.7 39.5 %copy-start.14 = (f32[128,2]{0,1:T(2,128)S(1)}, f32[128,2]{0,1:T(2,128)}, u32[]{:S(2)}) copy-start(f32[128,2]{0,1:T(2,128)} %param.22) | copy-start | bytes 3076
  131.7 39.5 %copy-start.15 = (f32[128,2]{0,1:T(2,128)S(1)}, f32[128,2]{0,1:T(2,128)}, u32[]{:S(2)}) copy-start(f32[128,2]{0,1:T(2,128)} %param.23) | copy-start | bytes 3076
  145.3 55.3 %copy-start.18 = (bf16[320,1024]{1,0:T(8,128)(2,1)S(1)}, bf16[320,1024]{1,0:T(8,128)(2,1)}, u32[]{:S(2)}) copy-start(bf16[320,1024]{1,0:T(8,128)(2,1)} %get-tuple-element.20) | copy-start | bytes 1966084
  145.3 60.9 %copy-start.17 = (bf16[320,1024]{1,0:T(8,128)(2,1)S(1)}, bf16[320,1024]{1,0:T(8,128)(2,1)}, u32[]{:S(2)}) copy-start(bf16[320,1024]{1,0:T(8,128)(2,1)} %get-tuple-element.21) | copy-start | bytes 1966084
  198.1 13.2 %collective-permute-start.11 = (bf16[64,40,128]{2,1,0:T(8,128)(2,1)S(1)}, bf16[64,40,128]{2,1,0:T(8,128)(2,1)}, u32[]{:S(2)}, u32[]{:S(2)}) collective-permute-start(bf16[64,40,128]{2,1,0:T(8,128)(2,1)S(1)} %all_to_all.26.refs_0_), channel_id=1, source_target_pairs={{0,128},{128,0},{64,192},{192,64},{1,129},{129,1},{65,193},{193,65... | collective-permute-start | bytes 1966088 | tf_op jit(solution)/shard_map/ppermute | solution.py:286
  200.5 16.6 %collective-permute-start.13 = (bf16[320,1024]{1,0:T(8,128)(2,1)S(1)}, bf16[320,1024]{1,0:T(8,128)(2,1)S(1)}, u32[]{:S(2)}, u32[]{:S(2)}) collective-permute-start(bf16[320,1024]{1,0:T(8,128)(2,1)S(1)} %copy-done.18), channel_id=1, source_target_pairs={{0,64},{64,0},{128,192},{192,128},{1,65},{65,1},{129,193},{193,129... | collective-permute-start | bytes 1966088 | tf_op jit(solution)/shard_map/ppermute | solution.py:282
  206.2 11.0 %collective-permute-start.14 = (bf16[320,1024]{1,0:T(8,128)(2,1)S(1)}, bf16[320,1024]{1,0:T(8,128)(2,1)S(1)}, u32[]{:S(2)}, u32[]{:S(2)}) collective-permute-start(bf16[320,1024]{1,0:T(8,128)(2,1)S(1)} %copy-done.17), channel_id=1, source_target_pairs={{0,64},{64,0},{128,192},{192,128},{1,65},{65,1},{129,193},{193,129... | collective-permute-start | bytes 1966088 | tf_op jit(solution)/shard_map/ppermute | solution.py:282
  206.3 21.0 %collective-permute-start.15 = (bf16[64,40,128]{2,1,0:T(8,128)(2,1)S(1)}, bf16[64,40,128]{2,1,0:T(8,128)(2,1)}, u32[]{:S(2)}, u32[]{:S(2)}) collective-permute-start(bf16[64,40,128]{2,1,0:T(8,128)(2,1)S(1)} %all_to_all.26.refs_0_), channel_id=1, source_target_pairs={{0,64},{64,0},{128,192},{192,128},{1,65},{65,1},{129,193},{193,129... | collective-permute-start | bytes 1966088 | tf_op jit(solution)/shard_map/ppermute | solution.py:282
  211.3 29.8 %collective-permute-start.12 = (bf16[64,40,128]{2,1,0:T(8,128)(2,1)}, bf16[64,40,128]{2,1,0:T(8,128)(2,1)}, u32[]{:S(2)}, u32[]{:S(2)}) collective-permute-start(bf16[64,40,128]{2,1,0:T(8,128)(2,1)} %collective-permute-done.11.refs_0_), channel_id=1, source_target_pairs={{0,64},{64,0},{128,192},{192,128},{1,65},{65,1},{129,193},{193,129... | collective-permute-start | bytes 1966088 | tf_op jit(solution)/shard_map/ppermute | solution.py:282
  218.9 8.4 %copy-start.5 = (bf16[1,512,1024]{2,1,0:T(8,128)(2,1)S(1)}, bf16[1,512,1024]{2,1,0:T(8,128)(2,1)}, u32[]{:S(2)}) copy-start(bf16[1,512,1024]{2,1,0:T(8,128)(2,1)} %refs_2_.3) | copy-start | bytes 3145732
  (10 other events, 12.3 us)

commit v2 on v1

--- a/solution.py
+++ b/solution.py
@@ -178,31 +178,37 @@
     )(rows, gate, up)
 
 
+def mix_in(flat, latent, mixed, where, scratch, gathered):
+    pieces = latent.shape[1] // LANES
+    scratch[...] = flat[...].astype(F32).reshape(scratch.shape)
+    for c in range(pieces):
+        gathered[:, c * LANES : (c + 1) * LANES] = load_flat(scratch, pieces, c).astype(BF16)
+    picked = [
+        jnp.dot(where[k], gathered[...], preferred_element_type=F32) * mixed[k] for k in range(2)
+    ]
+    return latent[...].astype(F32) + (picked[0] + picked[1])
+
+
+def student_body(
+    experts, capacity, flat, latent, s_routes, t_routes, mixing, output, s_where, t_where, scratch,
+    gathered,
+):
+    for routes, out in ((s_routes, s_where), (t_routes, t_where)):
+        first, second = places(routes[...], experts, capacity)
+        out[0] = first
+        out[1] = second
+    mixed = [column(mixing[...], k) for k in range(2)]
+    output[...] = mix_in(flat, latent, mixed, s_where, scratch, gathered)
+
+
 def combine_body(
-    experts, capacity, factor, s_flat, t_flat, s_latent, t_latent, s_routes, t_routes, s_mixing,
-    t_mixing, packed, scratch, gathered,
+    factor, flat, latent, student_out, s_where, t_where, s_mixing, t_mixing, packed, scratch,
+    gathered,
 ):
-    pieces = s_latent.shape[1] // LANES
-    found = []
-    for flat, latent, routes, mixing in (
-        (s_flat, s_latent, s_routes, s_mixing),
-        (t_flat, t_latent, t_routes, t_mixing),
-    ):
-        scratch[...] = flat[...].astype(F32).reshape(scratch.shape)
-        for c in range(pieces):
-            gathered[:, c * LANES : (c + 1) * LANES] = load_flat(scratch, pieces, c).astype(BF16)
-        where = places(routes[...], experts, capacity)
-        mixed = [column(mixing[...], k) for k in range(2)]
-        picked = [
-            jnp.dot(w, gathered[...], preferred_element_type=F32) * mixed[k]
-            for k, w in enumerate(where)
-        ]
-        found.append((latent[...].astype(F32) + (picked[0] + picked[1]), where, mixed))
-    cotangent = factor * (found[0][0] - found[1][0])
-    where, mixed = found[0][1:]
-    slots = [
-        turned_dot(w, (mixed[k] * cotangent).astype(BF16)) for k, w in enumerate(where)
-    ]
+    s_mixed, t_mixed = ([column(m[...], k) for k in range(2)] for m in (s_mixing, t_mixing))
+    target_out = mix_in(flat, latent, t_mixed, t_where, scratch, gathered)
+    cotangent = factor * (student_out[...] - target_out)
+    slots = [turned_dot(s_where[k], (s_mixed[k] * cotangent).astype(BF16)) for k in range(2)]
     store_flat(slots[0] + slots[1], scratch)
     packed[...] = scratch[...].reshape(packed.shape).astype(BF16)
 
@@ -348,15 +354,24 @@
     turned_rows, turned_hidden, by_gate, by_up = factors(rows, student_gate, student_up)
 
     factor = (experts / (top * tokens * groups * experts)) ** 0.5
+    room = (pltpu.VMEM(flat_shape, F32), pltpu.VMEM((slots, width), BF16))
+    where = jax.ShapeDtypeStruct((top, tokens, slots), BF16)
+    student_out, s_where, t_where = call(
+        functools.partial(student_body, experts, capacity),
+        (jax.ShapeDtypeStruct((tokens, width), F32), where, where),
+        room,
+        mib=62,
+        cost=4 * tokens * slots * width,
+    )(back_student, student_latent, student_routes, target_routes, student_mixing)
     slot_values = call(
-        functools.partial(combine_body, experts, capacity, factor),
+        functools.partial(combine_body, factor),
         jax.ShapeDtypeStruct(blocks_shape, BF16),
-        (pltpu.VMEM(flat_shape, F32), pltpu.VMEM((slots, width), BF16)),
-        mib=16,
+        room,
+        mib=62,
         cost=8 * tokens * slots * width,
     )(
-        back_student, back_target, student_latent, target_latent, student_routes,
-        target_routes, student_mixing, target_mixing,
+        back_target, target_latent, student_out, s_where, t_where, student_mixing,
+        target_mixing,
     )
     own_cot = to_experts(slot_values)
     far_cot = other_chip(own_cot)

time: 250 us -> 254 us (1.016)
  blocking collectives: 50.1 us -> 24.3 us
  waiting for transfers between devices: 59.7 us -> 73.6 us
  starting transfers between devices: 64.5 us -> 73.5 us
  Pallas kernels: 58.1 us -> 62.1 us
    all_to_all x2 -> x1, blocking collectives: 50.1 us -> 24.3 us  [to_experts(): lax.all_to_all(blocks, 'expert', split_axis=0, concat_axis=0, tiled=True)]
    all_to_all x3 -> x4, waiting for transfers between devices: 1.2 us -> 15 us  [to_experts(): lax.all_to_all(blocks, 'expert', split_axis=0, concat_axis=0, tiled=True)]
    all_to_all x3 -> x4, starting transfers between devices: 36.1 us -> 45.1 us  [to_experts(): lax.all_to_all(blocks, 'expert', split_axis=0, concat_axis=0, tiled=True)]
    pallas_call x1 -> x2, Pallas kernels: 2.67 us -> 6.74 us  [the longest x1 3.63 us: shards(): call(functools.partial(combine_body, factor), jax.ShapeDtypeStruct(blocks...]
    unnamed x46 -> x34, local copies, waits for them, and re-layouts: 10.8 us -> 11.6 us
  transfers between devices with their start and end apart: 19 -> 20, of which waited for: 8 -> 9; matrix products, arithmetic and copies ran while one was open for 2% -> 3% of each run, Pallas kernels for 18% -> 19%
where the time goes in v2:
time: 254 us; the launch traced here: 253 us
  waiting for transfers between devices  73.6 us (29%)
  starting transfers between devices  73.5 us (29%)
  Pallas kernels  62.1 us (24%)
  blocking collectives  24.3 us (10%)
  local copies, waits for them, and re-layouts  11.6 us (5%)
  other arithmetic  7.32 us (3%)
    ppermute x6, waiting for transfers between devices, other_chip(): return lax.ppermute(value, 'dp', ((0, 2), (2, 0), (1, 3), (3, 1)))  55.9 us
    all_to_all x4, starting transfers between devices, to_experts(): lax.all_to_all(blocks, 'expert', split_axis=0, concat_axis=0, tiled=True)  45.1 us
    pallas_call x4, Pallas kernels, forward(): call(forward_body, (jax.ShapeDtypeStruct((count, width), BF16), jax.Shape...  27 us
    all_to_all x1, blocking collectives, to_experts(): lax.all_to_all(blocks, 'expert', split_axis=0, concat_axis=0, tiled=True)  24.3 us
    pallas_call x2, Pallas kernels, backward(): call(functools.partial(backward_body, bool(earlier)), (jax.ShapeDtypeStru...  15.5 us
    ppermute x10, starting transfers between devices, other_core(): return lax.ppermute(value, 'dp', ((0, 1), (1, 0), (2, 3), (3, 2)))  15.4 us
    all_to_all x4, waiting for transfers between devices, to_experts(): lax.all_to_all(blocks, 'expert', split_axis=0, concat_axis=0, tiled=True)  15 us
    ppermute x6, starting transfers between devices, other_chip(): return lax.ppermute(value, 'dp', ((0, 2), (2, 0), (1, 3), (3, 1)))  13 us
  transfers between devices with their start and end apart: 20, of which 9 were waited for; matrix products, arithmetic and copies ran while one was open for 3% of the time, Pallas kernels for 19%

profile of v2, /device:TPU:1, one launch (start us, length us, event | category | flops | bytes accessed | tf_op | source)
XLA Modules:
  0.0 253.2 jit_solution(7264265747723777123)
XLA Ops:
  2.3 1.8 shard_map.142
  4.0 13.6 %all-to-all-start.2 = ((bf16[64,40,128]{2,1,0:T(8,128)(2,1)}), bf16[64,40,128]{2,1,0:T(8,128)(2,1)S(1)}, u32[]{:S(2)}, u32[]{:S(2)}) async-start(bf16[64,40,128]{2,1,0:T(8,128)(2,1)} %shard_map.142), calls=%async_computation.2 | async-start | bytes 1310720 | tf_op jit(solution)/shard_map/all_to_all | solution.py:284
  17.7 2.7 %collective-permute-start = (bf16[128,1024]{1,0:T(8,128)(2,1)}, bf16[128,1024]{1,0:T(8,128)(2,1)S(1)}, u32[]{:S(2)}, u32[]{:S(2)}) collective-permute-start(bf16[128,1024]{1,0:T(8,128)(2,1)} %latent.3), channel_id=1, source_target_pairs={{0,128},{128,0},{64,192},{192,64},{1,129},{129,1},{65,193},{193,65... | collective-permute-start | bytes 786440 | tf_op jit(solution)/shard_map/ppermute | solution.py:292
  20.7 9.3 %collective-permute-done.1.refs_3_ = s32[2,128]{1,0:T(2,128)S(1)} collective-permute-done((s32[2,128]{1,0:T(2,128)}, s32[2,128]{1,0:T(2,128)S(1)}, u32[]{:S(2)}, u32[]{:S(2)}) %collective-permute-start.1) | collective-permute-done | bytes 1056 | tf_op jit(solution)/shard_map/ppermute | solution.py:292
  31.6 2.7 %shard_map.139 = bf16[64,80,128]{2,1,0:T(8,128)(2,1)} custom-call(bf16[128,1024]{1,0:T(8,128)(2,1)S(1)} %copy-done.7, s32[2,128]{1,0:T(2,128)S(1)} %bitcast.6, bf16[128,1024]{1,0:T(8,128)(2,1)S(1)} %collective-permute-done.refs_2_, s32[2,128]{1,0:T(2,128)S(1)} %collective-permute-done.1.refs_3_), custom_call_target="tpu_custom_call" | custom-call | flops 83886080 | bytes 1048576 | tf_op jit(solution)/shard_map/pallas_call | solution.py:320
  35.5 12.2 %all-to-all-start = ((bf16[64,80,128]{2,1,0:T(8,128)(2,1)}), bf16[64,80,128]{2,1,0:T(8,128)(2,1)}, u32[]{:S(2)}, u32[]{:S(2)}) async-start(bf16[64,80,128]{2,1,0:T(8,128)(2,1)} %shard_map.139), calls=%async_computation | async-start | bytes 2621440 | tf_op jit(solution)/shard_map/all_to_all | solution.py:284
  49.8 2.4 collective-permute-start.9
  55.8 23.5 %collective-permute-done.9.flat = bf16[64,40,128]{2,1,0:T(8,128)(2,1)} collective-permute-done((bf16[64,40,128]{2,1,0:T(8,128)(2,1)S(1)}, bf16[64,40,128]{2,1,0:T(8,128)(2,1)}, u32[]{:S(2)}, u32[]{:S(2)}) %collective-permute-start.9) | collective-permute-done | bytes 655392 | tf_op jit(solution)/shard_map/ppermute | solution.py:292
  79.3 6.9 %shard_map.144 = (bf16[320,1024]{1,0:T(8,128)(2,1)}, bf16[64,40,128]{2,1,0:T(8,128)(2,1)}) custom-call(bf16[64,40,128]{2,1,0:T(8,128)(2,1)} %collective-permute-done.9.flat, bf16[1,1024,512]{2,1,0:T(8,128)(2,1)} %gate.9, bf16[1,1024,512]{2,1,0:T(8,128)(2,1)} %up.9, bf16[1,512,1024]{2,1,0:T(8,128)(2,1)} %refs_2_.3, bf16[1,1024,512]{2,1,0:T(8,128)(2,1)} %copy-done.14, ...), custom_call_target="tpu_custom_call" | custom-call | flops 2013265920 | bytes 1048576 | tf_op jit(solution)/shard_map/pallas_call | solution.py:122
  86.2 2.5 collective-permute-start.10
  89.9 7.1 %shard_map.143 = (bf16[320,1024]{1,0:T(8,128)(2,1)}, f32[64,40,128]{2,1,0:T(8,128)}) custom-call(bf16[64,40,128]{2,1,0:T(8,128)(2,1)} %copy-done.13, bf16[1,1024,512]{2,1,0:T(8,128)(2,1)} %gate.9, bf16[1,1024,512]{2,1,0:T(8,128)(2,1)} %up.9, bf16[1,512,1024]{2,1,0:T(8,128)(2,1)} %refs_2_.3, bf16[1,1024,512]{2,1,0:T(8,128)(2,1)} %copy-done.14, ...), custom_call_target="tpu_custom_call" | custom-call | flops 2013265920 | bytes 1048576 | tf_op jit(solution)/shard_map/pallas_call | solution.py:122
  97.1 6.4 %collective-permute-done.10 = bf16[64,40,128]{2,1,0:T(8,128)(2,1)S(1)} collective-permute-done((bf16[64,40,128]{2,1,0:T(8,128)(2,1)}, bf16[64,40,128]{2,1,0:T(8,128)(2,1)S(1)}, u32[]{:S(2)}, u32[]{:S(2)}) %collective-permute-start.10) | collective-permute-done | bytes 655392 | tf_op jit(solution)/shard_map/ppermute | solution.py:292
  103.5 2.3 add_convert_fusion
  105.8 10.3 %all-to-all-start.3 = ((bf16[64,40,128]{2,1,0:T(8,128)(2,1)}), bf16[64,40,128]{2,1,0:T(8,128)(2,1)S(1)}, u32[]{:S(2)}, u32[]{:S(2)}) async-start(bf16[64,40,128]{2,1,0:T(8,128)(2,1)} %add_convert_fusion), calls=%async_computation.3 | async-start | bytes 1310720 | tf_op jit(solution)/shard_map/all_to_all | solution.py:284
  116.1 6.4 %shard_map.141 = (bf16[320,1024]{1,0:T(8,128)(2,1)}, bf16[64,40,128]{2,1,0:T(8,128)(2,1)}) custom-call(bf16[64,80,128]{2,1,0:T(8,128)(2,1)} %all-to-all-done.flat, bf16[1,1024,512]{2,1,0:T(8,128)(2,1)} %gate.6, bf16[1,1024,512]{2,1,0:T(8,128)(2,1)} %up.6, bf16[1,512,1024]{2,1,0:T(8,128)(2,1)} %down.5, bf16[1,1024,512]{2,1,0:T(8,128)(2,1)} %collective-permute-done.2.gate2, ...), custom_call_target="tpu_custom_call" | custom-call | flops 2013265920 | bytes 1048576 | tf_op jit(solution)/shard_map/pallas_call | solution.py:122
  122.5 2.6 %collective-permute-start.5 = (bf16[64,40,128]{2,1,0:T(8,128)(2,1)}, bf16[64,40,128]{2,1,0:T(8,128)(2,1)S(1)}, u32[]{:S(2)}, u32[]{:S(2)}) collective-permute-start(bf16[64,40,128]{2,1,0:T(8,128)(2,1)} %get-tuple-element.20), channel_id=1, source_target_pairs={{0,128},{128,0},{64,192},{192,64},{1,129},{129,1},{65,193},{193,65... | collective-permute-start | bytes 1966088 | tf_op jit(solution)/shard_map/ppermute | solution.py:292
  125.1 6.6 %shard_map.140 = (bf16[320,1024]{1,0:T(8,128)(2,1)}, f32[64,40,128]{2,1,0:T(8,128)}) custom-call(bf16[64,80,128]{2,1,0:T(8,128)(2,1)} %all-to-all-done.flat, bf16[1,1024,512]{2,1,0:T(8,128)(2,1)} %gate.6, bf16[1,1024,512]{2,1,0:T(8,128)(2,1)} %up.6, bf16[1,512,1024]{2,1,0:T(8,128)(2,1)} %down.5, bf16[1,1024,512]{2,1,0:T(8,128)(2,1)} %collective-permute-done.2.gate2, ...), custom_call_target="tpu_custom_call" | custom-call | flops 2013265920 | bytes 1048576 | tf_op jit(solution)/shard_map/pallas_call | solution.py:122
  131.7 12.1 %collective-permute-done.5 = bf16[64,40,128]{2,1,0:T(8,128)(2,1)S(1)} collective-permute-done((bf16[64,40,128]{2,1,0:T(8,128)(2,1)}, bf16[64,40,128]{2,1,0:T(8,128)(2,1)S(1)}, u32[]{:S(2)}, u32[]{:S(2)}) %collective-permute-start.5) | collective-permute-done | bytes 655392 | tf_op jit(solution)/shard_map/ppermute | solution.py:292
  143.8 2.3 add_convert_fusion.1
  146.1 9.0 %all-to-all-start.1 = ((bf16[64,40,128]{2,1,0:T(8,128)(2,1)}), bf16[64,40,128]{2,1,0:T(8,128)(2,1)S(1)}, u32[]{:S(2)}, u32[]{:S(2)}) async-start(bf16[64,40,128]{2,1,0:T(8,128)(2,1)} %add_convert_fusion.1), calls=%async_computation.1 | async-start | bytes 1310720 | tf_op jit(solution)/shard_map/all_to_all | solution.py:284
  155.2 3.1 %shard_map.145 = (f32[128,1024]{1,0:T(8,128)}, bf16[2,128,320]{2,1,0:T(8,128)(2,1)}, bf16[2,128,320]{2,1,0:T(8,128)(2,1)}) custom-call(bf16[64,40,128]{2,1,0:T(8,128)(2,1)} %copy-done.11, bf16[128,1024]{1,0:T(8,128)(2,1)} %latent.2, s32[2,128]{1,0:T(2,128)} %bitcast.7, s32[2,128]{1,0:T(2,128)} %bitcast.5, f32[2,128]{1,0:T(2,128)} %bitcast.9), custom_call_target="tpu_custom_call" | custom-call | flops 167772160 | bytes 1048576 | tf_op jit(solution)/shard_map/pallas_call | solution.py:359
  158.3 13.8 %all-to-all-done.1.flat = bf16[64,40,128]{2,1,0:T(8,128)(2,1)S(1)} async-done(((bf16[64,40,128]{2,1,0:T(8,128)(2,1)}), bf16[64,40,128]{2,1,0:T(8,128)(2,1)S(1)}, u32[]{:S(2)}, u32[]{:S(2)}) %all-to-all-start.1) | async-done | bytes 655392 | tf_op jit(solution)/shard_map/all_to_all | solution.py:284
  172.9 3.6 %shard_map.146 = bf16[64,40,128]{2,1,0:T(8,128)(2,1)} custom-call(bf16[64,40,128]{2,1,0:T(8,128)(2,1)} %copy-done.12, bf16[128,1024]{1,0:T(8,128)(2,1)} %latent.3, f32[128,1024]{1,0:T(8,128)} %get-tuple-element.23.student_out, bf16[2,128,320]{2,1,0:T(8,128)(2,1)} %get-tuple-element.24.s_where, bf16[2,128,320]{2,1,0:T(8,128)(2,1)} %get-tuple-element.25.t_where, ...), custom_call_target="tpu_custom_call" | custom-call | flops 335544320 | bytes 1048576 | tf_op jit(solution)/shard_map/pallas_call | solution.py:366
  176.6 24.3 %all_to_all.25.refs_0_ = bf16[64,40,128]{2,1,0:T(8,128)(2,1)S(1)} all-to-all(bf16[64,40,128]{2,1,0:T(8,128)(2,1)} %shard_map.146), channel_id=1, replica_groups=mesh['dp'=4,'expert'=64] {'expert'}, dimensions={0} | all-to-all | bytes 1310720 | tf_op jit(solution)/shard_map/all_to_all | solution.py:284
  200.9 2.5 collective-permute-start.11
  203.4 5.6 %collective-permute-start.13 = (bf16[320,1024]{1,0:T(8,128)(2,1)}, bf16[320,1024]{1,0:T(8,128)(2,1)S(1)}, u32[]{:S(2)}, u32[]{:S(2)}) collective-permute-start(bf16[320,1024]{1,0:T(8,128)(2,1)} %get-tuple-element.26), channel_id=1, source_target_pairs={{0,64},{64,0},{128,192},{192,128},{1,65},{65,1},{129,193},{193,129... | collective-permute-start | bytes 1966088 | tf_op jit(solution)/shard_map/ppermute | solution.py:288
  209.5 4.6 %collective-permute-done.11.refs_0_ = bf16[64,40,128]{2,1,0:T(8,128)(2,1)} collective-permute-done((bf16[64,40,128]{2,1,0:T(8,128)(2,1)S(1)}, bf16[64,40,128]{2,1,0:T(8,128)(2,1)}, u32[]{:S(2)}, u32[]{:S(2)}) %collective-permute-start.11) | collective-permute-done | bytes 655392 | tf_op jit(solution)/shard_map/ppermute | solution.py:292
  214.1 5.9 %collective-permute-start.12 = (bf16[64,40,128]{2,1,0:T(8,128)(2,1)}, bf16[64,40,128]{2,1,0:T(8,128)(2,1)}, u32[]{:S(2)}, u32[]{:S(2)}) collective-permute-start(bf16[64,40,128]{2,1,0:T(8,128)(2,1)} %collective-permute-done.11.refs_0_), channel_id=1, source_target_pairs={{0,64},{64,0},{128,192},{192,128},{1,65},{65,1},{129,193},{193,129... | collective-permute-start | bytes 1966088 | tf_op jit(solution)/shard_map/ppermute | solution.py:288
  220.0 2.8 %pad_maximum_fusion.rows = bf16[1280,1024]{1,0:T(8,128)(2,1)} fusion(bf16[320,1024]{1,0:T(8,128)(2,1)S(1)} %collective-permute-done.14, bf16[320,1024]{1,0:T(8,128)(2,1)} %get-tuple-element.27, bf16[320,1024]{1,0:T(8,128)(2,1)S(1)} %collective-permute-done.13, bf16[320,1024]{1,0:T(8,128)(2,1)} %get-tuple-element.26), kind=kLoop, calls=%fused_computation | loop fusion | flops 10485760 | bytes 5242880 | tf_op jit(solution)/shard_map/concatenate | solution.py:353
  222.8 8.4 %shard_map.147 = (bf16[1024,1280]{1,0:T(8,128)(2,1)}, bf16[512,1280]{1,0:T(8,128)(2,1)}, f32[1280,512]{1,0:T(8,128)}, f32[1280,512]{1,0:T(8,128)}) custom-call(bf16[1280,1024]{1,0:T(8,128)(2,1)} %pad_maximum_fusion.rows, bf16[1,1024,512]{2,1,0:T(8,128)(2,1)} %gate.9, bf16[1,1024,512]{2,1,0:T(8,128)(2,1)} %up.9), custom_call_target="tpu_custom_call" | custom-call | flops 2684354560 | bytes 1048576 | tf_op jit(solution)/shard_map/pallas_call | solution.py:160
  237.7 7.3 %shard_map.148 = (f32[1,1024,512]{2,1,0:T(8,128)S(1)}, f32[1,1024,512]{2,1,0:T(8,128)S(1)}, f32[1,512,1024]{2,1,0:T(8,128)S(1)}) custom-call(bf16[64,40,128]{2,1,0:T(8,128)(2,1)S(1)} %all_to_all.25.refs_0_, bf16[64,40,128]{2,1,0:T(8,128)(2,1)} %collective-permute-done.15.refs_1_, bf16[1,512,1024]{2,1,0:T(8,128)(2,1)S(1)} %copy-done.5, ...), custom_call_target="tpu_custom_call" | custom-call | flops 2684354560 | bytes 1048576 | tf_op jit(solution)/shard_map/pallas_call | solution.py:260
  245.0 8.2 %shard_map.149 = (bf16[1,1024,512]{2,1,0:T(8,128)(2,1)}, bf16[1,1024,512]{2,1,0:T(8,128)(2,1)}, bf16[1,512,1024]{2,1,0:T(8,128)(2,1)}) custom-call(bf16[64,40,128]{2,1,0:T(8,128)(2,1)} %collective-permute-done.11.refs_0_, bf16[64,40,128]{2,1,0:T(8,128)(2,1)} %collective-permute-done.12.refs_1_, bf16[1,512,1024]{2,1,0:T(8,128)(2,1)S(1)} %copy-done.5, ...), custom_call_target="tpu_custom_call" | custom-call | flops 2684354560 | bytes 1048576 | tf_op jit(solution)/shard_map/pallas_call | solution.py:260
  (57 shorter events, 19.6 us)
Async XLA Ops:
  4.0 45.4 %copy-start.4 = (bf16[1,512,1024]{2,1,0:T(8,128)(2,1)S(1)}, bf16[1,512,1024]{2,1,0:T(8,128)(2,1)}, u32[]{:S(2)}) copy-start(bf16[1,512,1024]{2,1,0:T(8,128)(2,1)} %refs_2_.3) | copy-start | bytes 3145732
  4.0 31.5 %all-to-all-start.2 = ((bf16[64,40,128]{2,1,0:T(8,128)(2,1)}), bf16[64,40,128]{2,1,0:T(8,128)(2,1)S(1)}, u32[]{:S(2)}, u32[]{:S(2)}) async-start(bf16[64,40,128]{2,1,0:T(8,128)(2,1)} %shard_map.142), calls=%async_computation.2 | async-start | bytes 1310720 | tf_op jit(solution)/shard_map/all_to_all | solution.py:284
  17.7 12.4 %collective-permute-start = (bf16[128,1024]{1,0:T(8,128)(2,1)}, bf16[128,1024]{1,0:T(8,128)(2,1)S(1)}, u32[]{:S(2)}, u32[]{:S(2)}) collective-permute-start(bf16[128,1024]{1,0:T(8,128)(2,1)} %latent.3), channel_id=1, source_target_pairs={{0,128},{128,0},{64,192},{192,64},{1,129},{129,1},{65,193},{193,65... | collective-permute-start | bytes 786440 | tf_op jit(solution)/shard_map/ppermute | solution.py:292
  20.4 9.6 %collective-permute-start.1 = (s32[2,128]{1,0:T(2,128)}, s32[2,128]{1,0:T(2,128)S(1)}, u32[]{:S(2)}, u32[]{:S(2)}) collective-permute-start(s32[2,128]{1,0:T(2,128)} %bitcast.4), channel_id=1, source_target_pairs={{0,128},{128,0},{64,192},{192,64},{1,129},{129,1},{65,193},{193,65... | collective-permute-start | bytes 3080 | tf_op jit(solution)/shard_map/ppermute | solution.py:292
  35.5 50.7 %copy-start.13 = (bf16[64,40,128]{2,1,0:T(8,128)(2,1)}, bf16[64,40,128]{2,1,0:T(8,128)(2,1)S(1)}, u32[]{:S(2)}) copy-start(bf16[64,40,128]{2,1,0:T(8,128)(2,1)S(1)} %all-to-all-done.2.flat) | copy-start | bytes 1966084
  35.5 70.2 %all-to-all-start = ((bf16[64,80,128]{2,1,0:T(8,128)(2,1)}), bf16[64,80,128]{2,1,0:T(8,128)(2,1)}, u32[]{:S(2)}, u32[]{:S(2)}) async-start(bf16[64,80,128]{2,1,0:T(8,128)(2,1)} %shard_map.139), calls=%async_computation | async-start | bytes 2621440 | tf_op jit(solution)/shard_map/all_to_all | solution.py:284
  47.7 41.0 %copy-start.10 = (bf16[1,1024,512]{2,1,0:T(8,128)(2,1)S(1)}, bf16[1,1024,512]{2,1,0:T(8,128)(2,1)}, u32[]{:S(2)}) copy-start(bf16[1,1024,512]{2,1,0:T(8,128)(2,1)} %gate.6) | copy-start | bytes 3145732
  47.7 4.5 %collective-permute-start.6 = (bf16[1,1024,512]{2,1,0:T(8,128)(2,1)}, bf16[1,1024,512]{2,1,0:T(8,128)(2,1)S(1)}, u32[]{:S(2)}, u32[]{:S(2)}) collective-permute-start(bf16[1,1024,512]{2,1,0:T(8,128)(2,1)} %gate.9), channel_id=1, source_target_pairs={{0,64},{64,0},{128,192},{192,128},{1,65},{65,1},{129,193},{193,129... | collective-permute-start | bytes 3145736 | tf_op jit(solution)/shard_map/ppermute | solution.py:288
  49.3 4.0 %collective-permute-start.7 = (bf16[1,1024,512]{2,1,0:T(8,128)(2,1)}, bf16[1,1024,512]{2,1,0:T(8,128)(2,1)S(1)}, u32[]{:S(2)}, u32[]{:S(2)}) collective-permute-start(bf16[1,1024,512]{2,1,0:T(8,128)(2,1)} %up.9), channel_id=1, source_target_pairs={{0,64},{64,0},{128,192},{192,128},{1,65},{65,1},{129,193},{193,129... | collective-permute-start | bytes 3145736 | tf_op jit(solution)/shard_map/ppermute | solution.py:288
  49.4 5.4 %collective-permute-start.8 = (bf16[1,512,1024]{2,1,0:T(8,128)(2,1)S(1)}, bf16[1,512,1024]{2,1,0:T(8,128)(2,1)S(1)}, u32[]{:S(2)}, u32[]{:S(2)}) collective-permute-start(bf16[1,512,1024]{2,1,0:T(8,128)(2,1)S(1)} %copy-done.4), channel_id=1, source_target_pairs={{0,64},{64,0},{128,192},{192,128},{1,65},{65,1},{129,193},{193,129... | collective-permute-start | bytes 3145736 | tf_op jit(solution)/shard_map/ppermute | solution.py:288
  49.8 29.5 %collective-permute-start.9 = (bf16[64,40,128]{2,1,0:T(8,128)(2,1)S(1)}, bf16[64,40,128]{2,1,0:T(8,128)(2,1)}, u32[]{:S(2)}, u32[]{:S(2)}) collective-permute-start(bf16[64,40,128]{2,1,0:T(8,128)(2,1)S(1)} %all-to-all-done.2.flat), channel_id=1, source_target_pairs={{0,128},{128,0},{64,192},{192,64},{1,129},{129,1},{65,193},{193,65... | collective-permute-start | bytes 1966088 | tf_op jit(solution)/shard_map/ppermute | solution.py:292
  52.2 2.6 %copy-start.14 = (bf16[1,1024,512]{2,1,0:T(8,128)(2,1)}, bf16[1,1024,512]{2,1,0:T(8,128)(2,1)S(1)}, u32[]{:S(2)}) copy-start(bf16[1,1024,512]{2,1,0:T(8,128)(2,1)S(1)} %collective-permute-done.6.gate2) | copy-start | bytes 3145732
  53.3 1.5 copy-start.15
  54.8 1.0 copy-start.16
  86.2 17.3 %collective-permute-start.10 = (bf16[64,40,128]{2,1,0:T(8,128)(2,1)}, bf16[64,40,128]{2,1,0:T(8,128)(2,1)S(1)}, u32[]{:S(2)}, u32[]{:S(2)}) collective-permute-start(bf16[64,40,128]{2,1,0:T(8,128)(2,1)} %get-tuple-element.22), channel_id=1, source_target_pairs={{0,128},{128,0},{64,192},{192,64},{1,129},{129,1},{65,193},{193,65... | collective-permute-start | bytes 1966088 | tf_op jit(solution)/shard_map/ppermute | solution.py:292
  88.7 27.4 %collective-permute-start.2 = (bf16[1,1024,512]{2,1,0:T(8,128)(2,1)S(1)}, bf16[1,1024,512]{2,1,0:T(8,128)(2,1)}, u32[]{:S(2)}, u32[]{:S(2)}) collective-permute-start(bf16[1,1024,512]{2,1,0:T(8,128)(2,1)S(1)} %copy-done.10), channel_id=1, source_target_pairs={{0,64},{64,0},{128,192},{192,128},{1,65},{65,1},{129,193},{193,129... | collective-permute-start | bytes 3145736 | tf_op jit(solution)/shard_map/ppermute | solution.py:288
  89.4 26.7 %collective-permute-start.3 = (bf16[1,1024,512]{2,1,0:T(8,128)(2,1)}, bf16[1,1024,512]{2,1,0:T(8,128)(2,1)}, u32[]{:S(2)}, u32[]{:S(2)}) collective-permute-start(bf16[1,1024,512]{2,1,0:T(8,128)(2,1)} %up.6), channel_id=1, source_target_pairs={{0,64},{64,0},{128,192},{192,128},{1,65},{65,1},{129,193},{193,129... | collective-permute-start | bytes 3145736 | tf_op jit(solution)/shard_map/ppermute | solution.py:288
  89.4 26.7 %collective-permute-start.4 = (bf16[1,512,1024]{2,1,0:T(8,128)(2,1)}, bf16[1,512,1024]{2,1,0:T(8,128)(2,1)}, u32[]{:S(2)}, u32[]{:S(2)}) collective-permute-start(bf16[1,512,1024]{2,1,0:T(8,128)(2,1)} %down.5), channel_id=1, source_target_pairs={{0,64},{64,0},{128,192},{192,128},{1,65},{65,1},{129,193},{193,129... | collective-permute-start | bytes 3145736 | tf_op jit(solution)/shard_map/ppermute | solution.py:288
  105.8 40.4 %all-to-all-start.3 = ((bf16[64,40,128]{2,1,0:T(8,128)(2,1)}), bf16[64,40,128]{2,1,0:T(8,128)(2,1)S(1)}, u32[]{:S(2)}, u32[]{:S(2)}) async-start(bf16[64,40,128]{2,1,0:T(8,128)(2,1)} %add_convert_fusion), calls=%async_computation.3 | async-start | bytes 1310720 | tf_op jit(solution)/shard_map/all_to_all | solution.py:284
  122.5 21.3 %collective-permute-start.5 = (bf16[64,40,128]{2,1,0:T(8,128)(2,1)}, bf16[64,40,128]{2,1,0:T(8,128)(2,1)S(1)}, u32[]{:S(2)}, u32[]{:S(2)}) collective-permute-start(bf16[64,40,128]{2,1,0:T(8,128)(2,1)} %get-tuple-element.20), channel_id=1, source_target_pairs={{0,128},{128,0},{64,192},{192,64},{1,129},{129,1},{65,193},{193,65... | collective-permute-start | bytes 1966088 | tf_op jit(solution)/shard_map/ppermute | solution.py:292
  146.1 9.0 %copy-start.11 = (bf16[64,40,128]{2,1,0:T(8,128)(2,1)}, bf16[64,40,128]{2,1,0:T(8,128)(2,1)S(1)}, u32[]{:S(2)}) copy-start(bf16[64,40,128]{2,1,0:T(8,128)(2,1)S(1)} %all-to-all-done.3.flat) | copy-start | bytes 1966084
  146.1 26.0 %all-to-all-start.1 = ((bf16[64,40,128]{2,1,0:T(8,128)(2,1)}), bf16[64,40,128]{2,1,0:T(8,128)(2,1)S(1)}, u32[]{:S(2)}, u32[]{:S(2)}) async-start(bf16[64,40,128]{2,1,0:T(8,128)(2,1)} %add_convert_fusion.1), calls=%async_computation.1 | async-start | bytes 1310720 | tf_op jit(solution)/shard_map/all_to_all | solution.py:284
  200.9 13.2 %collective-permute-start.11 = (bf16[64,40,128]{2,1,0:T(8,128)(2,1)S(1)}, bf16[64,40,128]{2,1,0:T(8,128)(2,1)}, u32[]{:S(2)}, u32[]{:S(2)}) collective-permute-start(bf16[64,40,128]{2,1,0:T(8,128)(2,1)S(1)} %all_to_all.25.refs_0_), channel_id=1, source_target_pairs={{0,128},{128,0},{64,192},{192,64},{1,129},{129,1},{65,193},{193,65... | collective-permute-start | bytes 1966088 | tf_op jit(solution)/shard_map/ppermute | solution.py:292
  203.4 16.6 %collective-permute-start.13 = (bf16[320,1024]{1,0:T(8,128)(2,1)}, bf16[320,1024]{1,0:T(8,128)(2,1)S(1)}, u32[]{:S(2)}, u32[]{:S(2)}) collective-permute-start(bf16[320,1024]{1,0:T(8,128)(2,1)} %get-tuple-element.26), channel_id=1, source_target_pairs={{0,64},{64,0},{128,192},{192,128},{1,65},{65,1},{129,193},{193,129... | collective-permute-start | bytes 1966088 | tf_op jit(solution)/shard_map/ppermute | solution.py:288
  209.0 11.0 %collective-permute-start.14 = (bf16[320,1024]{1,0:T(8,128)(2,1)}, bf16[320,1024]{1,0:T(8,128)(2,1)S(1)}, u32[]{:S(2)}, u32[]{:S(2)}) collective-permute-start(bf16[320,1024]{1,0:T(8,128)(2,1)} %get-tuple-element.27), channel_id=1, source_target_pairs={{0,64},{64,0},{128,192},{192,128},{1,65},{65,1},{129,193},{193,129... | collective-permute-start | bytes 1966088 | tf_op jit(solution)/shard_map/ppermute | solution.py:288
  209.0 22.1 %collective-permute-start.15 = (bf16[64,40,128]{2,1,0:T(8,128)(2,1)S(1)}, bf16[64,40,128]{2,1,0:T(8,128)(2,1)}, u32[]{:S(2)}, u32[]{:S(2)}) collective-permute-start(bf16[64,40,128]{2,1,0:T(8,128)(2,1)S(1)} %all_to_all.25.refs_0_), channel_id=1, source_target_pairs={{0,64},{64,0},{128,192},{192,128},{1,65},{65,1},{129,193},{193,129... | collective-permute-start | bytes 1966088 | tf_op jit(solution)/shard_map/ppermute | solution.py:288
  214.1 30.8 %collective-permute-start.12 = (bf16[64,40,128]{2,1,0:T(8,128)(2,1)}, bf16[64,40,128]{2,1,0:T(8,128)(2,1)}, u32[]{:S(2)}, u32[]{:S(2)}) collective-permute-start(bf16[64,40,128]{2,1,0:T(8,128)(2,1)} %collective-permute-done.11.refs_0_), channel_id=1, source_target_pairs={{0,64},{64,0},{128,192},{192,128},{1,65},{65,1},{129,193},{193,129... | collective-permute-start | bytes 1966088 | tf_op jit(solution)/shard_map/ppermute | solution.py:288
  222.8 8.4 %copy-start.5 = (bf16[1,512,1024]{2,1,0:T(8,128)(2,1)S(1)}, bf16[1,512,1024]{2,1,0:T(8,128)(2,1)}, u32[]{:S(2)}) copy-start(bf16[1,512,1024]{2,1,0:T(8,128)(2,1)} %refs_2_.3) | copy-start | bytes 3145732
  231.1 1.7 copy-start
  232.9 1.7 copy-start.1
  234.6 1.7 copy-start.2
  236.4 1.3 copy-start.3
  (5 other events, 4.1 us)
